TPU v7x, 32 devices: a whole 2x2x4 slice. The times are simulated.
32 devices in a mesh: parts: 2 (over y), gz: 4 (over z), shot: 4 (over x, core).
Axes of the slice: x: 2, y: 2, z: 4, core: 2. Of those that a mesh axis runs over, the one named last changes fastest.
Arguments:
- wavefields: float32 [8, 2, 9, 16, 32, 128], P(('parts', 'shot'), None, None, 'gz'), parts along dimension 0, may hold values from -6 to 6
- earth_model: float32 [6, 16, 32, 128], P('parts', 'gz'), parts along dimension 0, may hold values from 0.4 to 1.6
- source_depth: int32 [8], P(('parts', 'shot')), parts along dimension 0, may hold values from 0 to 15
- source_column: int32 [8], P(('parts', 'shot')), parts along dimension 0, may hold values from 0 to 4095
- wavelet: float32 [8, 8], P(('parts', 'shot')), parts along dimension 0, may hold values from -30 to 30
- receiver_depth: int32 [8, 64], P(('parts', 'shot')), parts along dimension 0, may hold values from 0 to 15
- receiver_column: int32 [8, 64], P(('parts', 'shot')), parts along dimension 0, may hold values from 0 to 4095
- traces: float32 [8, 8, 64], P(('parts', 'shot')), parts along dimension 0, may hold values from -30 to 30
Outputs:
- images: float32 [4, 16, 32, 128], P('parts', 'gz'), parts along dimension 0
There are 2 independent parts, one for each index of `parts`. A program takes and returns all parts, laid end to end along the dimension named above; each array names one. Nothing has to cross between parts.
All inputs are finite; a program needn't handle non-finite values.
Results may differ from a plain program's by a relative error of at most 0.00002.
Values sent between devices are 32-bit elements; how exact they have to be, the bound alone decides.
A program may use at most 64 MiB of HBM per device.

v0:
```python
import functools

import jax
import jax.numpy as jnp
from jax import lax
from jax.experimental import pallas as pl
from jax.experimental.pallas import tpu as pltpu
from jax.sharding import PartitionSpec as P

time_step = 0.15
VX, VY, VZ, SXX, SYY, SZZ, SXY, SXZ, SYZ = range(9)
MESH = pl.DeviceIdType.MESH


def kernel(
    gz_count,
    shot_count,
    wave_hbm,
    earth_hbm,
    src_depth_hbm,
    src_column_hbm,
    wavelet_hbm,
    rec_depth_hbm,
    rec_column_hbm,
    traces_hbm,
    out,
    state,
    earth,
    low0,
    high0,
    earth_low,
    earth_high,
    low,
    high,
    send_low,
    send_high,
    inject,
    press,
    image,
    parts_in,
    own,
    src_depth,
    src_column,
    wavelet,
    rec_depth,
    rec_column,
    traces,
    load_sem,
    init_send,
    init_recv,
    low_send,
    low_recv,
    high_send,
    high_recv,
    img_send,
    img_recv,
    turn,
):
    planes, nx, ny = state.shape[2:]
    steps = traces.shape[0]
    h = time_step
    gz = lax.axis_index("gz")
    shot = lax.axis_index("shot")
    has_low = gz > 0
    has_high = gz < gz_count - 1

    load_wave = [
        pltpu.make_async_copy(wave_hbm.at[0, w], state.at[w], load_sem.at[w]) for w in range(2)
    ]
    load_earth = pltpu.make_async_copy(earth_hbm, earth, load_sem.at[2])
    small = [
        pltpu.make_async_copy(src, dst, load_sem.at[3 + i])
        for i, (src, dst) in enumerate(
            (
                (traces_hbm.at[0], traces),
                (rec_depth_hbm, rec_depth),
                (rec_column_hbm, rec_column),
                (src_depth_hbm, src_depth),
                (src_column_hbm, src_column),
                (wavelet_hbm, wavelet),
            )
        )
    ]
    for copy in small + [load_earth] + load_wave:
        copy.start()

    barrier = pltpu.get_barrier_semaphore()

    @pl.when(has_low)
    def _():
        pl.semaphore_signal(barrier, inc=1, device_id={"gz": gz - 1}, device_id_type=MESH)

    @pl.when(has_high)
    def _():
        pl.semaphore_signal(barrier, inc=1, device_id={"gz": gz + 1}, device_id_type=MESH)

    for k in range(1, shot_count):
        peer = lax.rem(shot + k, shot_count)
        pl.semaphore_signal(barrier, inc=1, device_id={"shot": peer}, device_id_type=MESH)

    low_peers = (gz + gz_count - 1) // gz_count
    high_peers = (2 * gz_count - 2 - gz) // gz_count
    pl.semaphore_wait(barrier, low_peers + high_peers + shot_count - 1)

    def remote(src, dst, sem, axis_to):
        return pltpu.make_async_remote_copy(
            src_ref=src,
            dst_ref=dst,
            send_sem=init_send.at[sem],
            recv_sem=init_recv.at[sem],
            device_id={"gz": axis_to},
            device_id_type=MESH,
        )

    last = planes - 1
    down = {
        w: [
            remote(wave_hbm.at[0, w, pl.ds(SXZ, 2), last], low0.at[w, pl.ds(2, 2)], 6 * w, gz + 1),
            remote(wave_hbm.at[0, w, SZZ, last], low0.at[w, 1], 6 * w + 1, gz + 1),
            remote(wave_hbm.at[0, w, VZ, last], low0.at[w, 0], 6 * w + 2, gz + 1),
        ]
        for w in range(2)
    }
    down_earth = remote(earth_hbm.at[0, last], earth_low, 12, gz + 1)
    up = {
        w: [
            remote(wave_hbm.at[0, w, pl.ds(SXX, 6), 0], high0.at[w, pl.ds(SXX, 6)], 6 * w + 3, gz - 1),
            remote(wave_hbm.at[0, w, pl.ds(VX, 2), 0], high0.at[w, pl.ds(VX, 2)], 6 * w + 4, gz - 1),
        ]
        for w in range(2)
    }
    up_earth = remote(earth_hbm.at[:, 0], earth_high, 13, gz - 1)
    down_all = down[0] + [down_earth] + down[1]
    up_all = up[0] + [up_earth] + up[1]

    def start_first():
        @pl.when(has_high)
        def _():
            for copy in down_all:
                copy.start()

        @pl.when(has_low)
        def _():
            for copy in up_all:
                copy.start()

    paired = shot_count % 2 == 0
    even = lax.rem(shot, 2) == 0
    if paired:
        pl.when(even)(start_first)
    else:
        start_first()

    @pl.when(jnp.logical_not(has_low))
    def _():
        low0[...] = jnp.zeros_like(low0)
        low[...] = jnp.zeros_like(low)
        earth_low[...] = jnp.zeros_like(earth_low)

    @pl.when(jnp.logical_not(has_high))
    def _():
        high0[...] = jnp.zeros_like(high0)
        high[...] = jnp.zeros_like(high)
        earth_high[...] = jnp.zeros_like(earth_high)

    image[...] = jnp.zeros_like(image)

    for copy in small:
        copy.wait()
    offset = gz * planes
    receivers = traces.shape[1]
    column = rec_column[...]
    depth = rec_depth[...] - offset
    row_ids = lax.broadcasted_iota(jnp.int32, (nx, receivers), 0) * ny
    past = column - row_ids
    on_row = (past >= 0) & (past < ny)
    row_hot = jnp.concatenate(
        [jnp.where(on_row & (depth == p), h, 0.0) for p in range(-1, planes)], axis=0
    )
    col_ids = lax.broadcasted_iota(jnp.int32, (ny, receivers), 0)
    col_hot = jnp.where((column & (ny - 1)) == col_ids, 1.0, 0.0)

    def fill(n, carry):
        inject[n] = lax.dot_general(
            row_hot * traces[pl.ds(n, 1), :],
            col_hot,
            (((1,), (1,)), ((), ())),
            precision=lax.Precision.HIGHEST,
            preferred_element_type=jnp.float32,
        ).reshape(planes + 1, nx, ny)
        return carry

    lax.fori_loop(0, steps, fill, 0)

    if paired:

        @pl.when(even)
        def _():
            @pl.when(has_high)
            def _():
                for copy in down_all:
                    copy.wait_send()

            @pl.when(has_low)
            def _():
                for copy in up_all:
                    copy.wait_send()

            pl.semaphore_signal(turn, inc=1, device_id={"shot": shot + 1}, device_id_type=MESH)

        @pl.when(jnp.logical_not(even))
        def _():
            pl.semaphore_wait(turn, 1)
            start_first()

    rows = lax.broadcasted_iota(jnp.int32, (nx, ny), 0)
    lanes = lax.broadcasted_iota(jnp.int32, (nx, ny), 1)
    cells = rows * ny + lanes

    def fx(a):
        return jnp.where(rows == nx - 1, 0.0, pltpu.roll(a, nx - 1, 0)) - a

    def bx(a):
        return a - jnp.where(rows == 0, 0.0, pltpu.roll(a, 1, 0))

    def fy(a):
        return jnp.where(lanes == ny - 1, 0.0, pltpu.roll(a, ny - 1, 1)) - a

    def by(a):
        return a - jnp.where(lanes == 0, 0.0, pltpu.roll(a, 1, 1))

    src_at = src_depth[0] - offset
    src_cell = src_column[0]

    def source_term(plane, n):
        cell = jnp.where(src_at == plane, src_cell, -1)
        return jnp.where(cells == cell, h * wavelet[0, n], 0.0)

    load_earth.wait()
    earth[...] = earth[...] * h

    def sends(w, n):
        to_high = pltpu.make_async_remote_copy(
            src_ref=send_low.at[w, n],
            dst_ref=low.at[w, n],
            send_sem=low_send.at[w, n],
            recv_sem=low_recv.at[w, n],
            device_id={"gz": gz + 1},
            device_id_type=MESH,
        )
        to_low = pltpu.make_async_remote_copy(
            src_ref=send_high.at[w, n],
            dst_ref=high.at[w, n],
            send_sem=high_send.at[w, n],
            recv_sem=high_recv.at[w, n],
            device_id={"gz": gz - 1},
            device_id_type=MESH,
        )
        return to_high, to_low

    def half(w, n, first, final):
        if first:
            load_wave[w].wait()

            @pl.when(has_low)
            def _():
                for copy in down[w]:
                    copy.wait_recv()
                if w == 0:
                    down_earth.wait_recv()

            @pl.when(has_high)
            def _():
                for copy in up[w]:
                    copy.wait_recv()
                if w == 0:
                    up_earth.wait_recv()

            szz_m, sxz_m, syz_m = (low0[w, i] for i in (1, 2, 3))
            sxz_p, syz_p = high0[w, SXZ], high0[w, SYZ]
        else:
            to_high, to_low = sends(w, n - 1)

            @pl.when(has_high)
            def _():
                to_low.wait_recv()

            @pl.when(has_low)
            def _():
                to_high.wait_recv()

            szz_m, sxz_m, syz_m = (low[w, n - 1, i] for i in range(3))
            vz_p, sxz_p, syz_p = (high[w, n - 1, i] for i in range(3))
            hlam = h * earth_high[1]
            hmu = h * earth_high[2]
            vx_p, vy_p = high0[w, VX], high0[w, VY]
            ex, ey, ez = bx(vx_p), by(vy_p), vz_p - state[w, VZ, last]
            spread = hlam * (ex + ey + ez)
            if w == 0:
                spread = spread + source_term(planes, n - 1)
            high0[w, SXX] += spread + 2.0 * hmu * ex
            high0[w, SYY] += spread + 2.0 * hmu * ey
            high0[w, SZZ] += spread + 2.0 * hmu * ez
            high0[w, SXY] += hmu * (fy(vx_p) + fx(vy_p))

        term = h * earth_low[...] * (bx(sxz_m) + by(syz_m) + (state[w, SZZ, 0] - szz_m))
        if w == 1:
            term = term + inject[n, 0]
        low0[w, 0] += term
        for p in range(planes):
            hb = earth[0, p]
            sxz, syz, szz, sxy = (state[w, i, p] for i in (SXZ, SYZ, SZZ, SXY))
            sxz_b = sxz_m if p == 0 else state[w, SXZ, p - 1]
            syz_b = syz_m if p == 0 else state[w, SYZ, p - 1]
            szz_f = high0[w, SZZ] if p == last else state[w, SZZ, p + 1]
            state[w, VX, p] += hb * (fx(state[w, SXX, p]) + by(sxy) + (sxz - sxz_b))
            state[w, VY, p] += hb * (bx(sxy) + fy(state[w, SYY, p]) + (syz - syz_b))
            term = hb * (bx(sxz) + by(syz) + (szz_f - szz))
            if w == 1:
                term = term + inject[n, p + 1]
            state[w, VZ, p] += term
        hb = h * earth_high[0]
        sxy = high0[w, SXY]
        high0[w, VX] += hb * (fx(high0[w, SXX]) + by(sxy) + (sxz_p - state[w, SXZ, last]))
        high0[w, VY] += hb * (bx(sxy) + fy(high0[w, SYY]) + (syz_p - state[w, SYZ, last]))

        def stress(p):
            vx, vy, vz = (state[w, i, p] for i in (VX, VY, VZ))
            vz_b = low0[w, 0] if p == 0 else state[w, VZ, p - 1]
            hmu = earth[2, p]
            ex, ey, ez = bx(vx), by(vy), vz - vz_b
            spread = earth[1, p] * (ex + ey + ez)
            if w == 0:
                spread = spread + source_term(p, n)
            mu2 = 2.0 * hmu
            sxx = state[w, SXX, p] + (spread + mu2 * ex)
            syy = state[w, SYY, p] + (spread + mu2 * ey)
            szz = state[w, SZZ, p] + (spread + mu2 * ez)
            pressure = (sxx + syy + szz) * (1.0 / 3.0)
            if not final:
                state[w, SXX, p] = sxx
                state[w, SYY, p] = syy
                state[w, SZZ, p] = szz
            if w == 1 or not final:
                vx_f = high0[w, VX] if p == last else state[w, VX, p + 1]
                vy_f = high0[w, VY] if p == last else state[w, VY, p + 1]
                vxz, vyz = vx_f - vx, vy_f - vy
                vzx, vzy, vxy, vyx = fx(vz), fy(vz), fy(vx), fx(vy)
            if not final:
                sxz = state[w, SXZ, p] + hmu * (vxz + vzx)
                syz = state[w, SYZ, p] + hmu * (vyz + vzy)
                state[w, SXY, p] += hmu * (vxy + vyx)
                state[w, SXZ, p] = sxz
                state[w, SYZ, p] = syz
                if p == 0:
                    send_high[w, n, 0] = vz
                    send_high[w, n, 1] = sxz
                    send_high[w, n, 2] = syz
                if p == last:
                    send_low[w, n, 0] = szz
                    send_low[w, n, 1] = sxz
                    send_low[w, n, 2] = syz
            if w == 0:
                press[p] = pressure
            else:
                rotation = (vzy - vyz) + (vxz - vzx) + (vyx - vxy)
                image[pl.ds(p * nx, nx), :] += press[p] * pressure
                image[pl.ds((planes + p) * nx, nx), :] += press[p] * rotation

        edge = sorted({0, last})
        for p in edge:
            stress(p)
        if not final:
            to_high, to_low = sends(w, n)

            @pl.when(has_low)
            def _():
                to_low.start()

            @pl.when(has_high)
            def _():
                to_high.start()

        for p in range(planes):
            if p not in edge:
                stress(p)

    def step(n, first, final):
        half(0, n, first, final)
        half(1, n, first, final)

    step(0, True, steps == 1)
    if steps > 2:

        def body(n, carry):
            step(n, False, False)
            return carry

        lax.fori_loop(1, steps - 1, body, 0)
    if steps > 1:
        step(steps - 1, False, True)

    total = image.shape[0]
    chunk = total // shot_count
    scale = 1.0 / steps

    def span(index):
        return pl.ds(pl.multiple_of(index * chunk, 8), chunk)

    scatter = []
    for k in range(1, shot_count):
        peer = lax.rem(shot + k, shot_count)
        copy = pltpu.make_async_remote_copy(
            src_ref=image.at[span(peer)],
            dst_ref=parts_in.at[k - 1],
            send_sem=img_send.at[0, k - 1],
            recv_sem=img_recv.at[0, k - 1],
            device_id={"shot": peer},
            device_id_type=MESH,
        )
        copy.start()
        scatter.append(copy)
    acc = image[span(shot), :]
    for k in range(1, shot_count):
        scatter[k - 1].wait_recv()
        acc = acc + parts_in[k - 1]
    acc = acc * scale
    own[...] = acc
    gather = []
    for k in range(1, shot_count):
        peer = lax.rem(shot + k, shot_count)
        copy = pltpu.make_async_remote_copy(
            src_ref=own,
            dst_ref=out.at[span(shot)],
            send_sem=img_send.at[1, k - 1],
            recv_sem=img_recv.at[1, k - 1],
            device_id={"shot": peer},
            device_id_type=MESH,
        )
        copy.start()
        gather.append(copy)
    out[span(shot), :] = acc

    late = jnp.logical_not(even) if paired else shot >= 0

    @pl.when(has_high & late)
    def _():
        for copy in down_all:
            copy.wait_send()

    @pl.when(has_low & late)
    def _():
        for copy in up_all:
            copy.wait_send()

    def drain(n, carry):
        for w in range(2):
            to_high, to_low = sends(w, n)

            @pl.when(has_high)
            def _():
                to_high.wait_send()

            @pl.when(has_low)
            def _():
                to_low.wait_send()

        return carry

    lax.fori_loop(0, steps - 1, drain, 0)
    for copy in scatter:
        copy.wait_send()
    for copy in gather:
        copy.wait()


def on_device(
    gz_count,
    shot_count,
    wavefields,
    earth_model,
    source_depth,
    source_column,
    wavelet,
    receiver_depth,
    receiver_column,
    traces,
):
    planes, nx, ny = wavefields.shape[3:]
    steps = wavelet.shape[1]
    slots = max(steps - 1, 1)
    rows = 2 * planes * nx
    peers = max(shot_count - 1, 1)
    f32 = jnp.float32
    vmem = pl.BlockSpec(memory_space=pltpu.VMEM)
    hbm = pl.BlockSpec(memory_space=pl.ANY)
    dma = pltpu.SemaphoreType.DMA
    summed = pl.pallas_call(
        functools.partial(kernel, gz_count, shot_count),
        out_shape=jax.ShapeDtypeStruct((rows, ny), f32),
        in_specs=[hbm] * 8,
        out_specs=vmem,
        scratch_shapes=[
            pltpu.VMEM((2, 9, planes, nx, ny), f32),
            pltpu.VMEM((3, planes, nx, ny), f32),
            pltpu.VMEM((2, 4, nx, ny), f32),
            pltpu.VMEM((2, 9, nx, ny), f32),
            pltpu.VMEM((nx, ny), f32),
            pltpu.VMEM((3, nx, ny), f32),
            pltpu.VMEM((2, slots, 3, nx, ny), f32),
            pltpu.VMEM((2, slots, 3, nx, ny), f32),
            pltpu.VMEM((2, slots, 3, nx, ny), f32),
            pltpu.VMEM((2, slots, 3, nx, ny), f32),
            pltpu.VMEM((steps, planes + 1, nx, ny), f32),
            pltpu.VMEM((planes, nx, ny), f32),
            pltpu.VMEM((rows, ny), f32),
            pltpu.VMEM((peers, rows // shot_count, ny), f32),
            pltpu.VMEM((rows // shot_count, ny), f32),
            pltpu.SMEM(source_depth.shape, jnp.int32),
            pltpu.SMEM(source_column.shape, jnp.int32),
            pltpu.SMEM(wavelet.shape, f32),
            pltpu.VMEM(receiver_depth.shape, jnp.int32),
            pltpu.VMEM(receiver_column.shape, jnp.int32),
            pltpu.VMEM(traces.shape[1:], f32),
            dma((9,)),
            dma((14,)),
            dma((14,)),
            dma((2, slots)),
            dma((2, slots)),
            dma((2, slots)),
            dma((2, slots)),
            dma((2, peers)),
            dma((2, peers)),
            pltpu.SemaphoreType.REGULAR,
        ],
        compiler_params=pltpu.CompilerParams(collective_id=0, has_side_effects=True),
    )(
        wavefields,
        earth_model,
        source_depth,
        source_column,
        wavelet,
        receiver_depth,
        receiver_column,
        traces,
    )
    return summed.reshape(2, planes, nx, ny)


def solution(mesh):
    placed = (
        P(("parts", "shot"), None, None, "gz", None, None),
        P("parts", "gz", None, None),
        P(("parts", "shot")),
        P(("parts", "shot")),
        P(("parts", "shot"), None),
        P(("parts", "shot"), None),
        P(("parts", "shot"), None),
        P(("parts", "shot"), None, None),
    )
    return jax.shard_map(
        functools.partial(on_device, mesh.shape["gz"], mesh.shape["shot"]),
        mesh=mesh,
        in_specs=placed,
        out_specs=P("parts", "gz", None, None),
        check_vma=False,
    )
```

profile of v0, /device:TPU:0, one launch (start us, length us, event | category | flops | bytes accessed | tf_op | source)
XLA Modules:
  0.0 46.3 jit_solution(18437812950495126130)
XLA Ops:
  1.3 43.4 %shard_map.82 = f32[256,128]{1,0:T(8,128)} custom-call(f32[1,2,9,4,32,128]{5,4,3,2,1,0:T(8,128)} %wave_hbm.1, f32[3,4,32,128]{3,2,1,0:T(8,128)} %earth_hbm.1, s32[1]{0:T(128)S(6)} %copy.10.src_depth_hbm, s32[1]{0:T(128)S(6)} %copy.11.src_column_hbm, f32[1,8]{1,0:T(1,128)} %wavelet_hbm.1, s32[1,64]{1,0:T(1,128)} %rec_depth_hbm.1, s32[1,64]{1,0:T(1,128)} %rec_column_hbm.1, ...), custom_call_target="tpu_custom_call" | custom-call | tf_op jit(solution)/shard_map/pallas_call | solution.py:498
  44.7 1.6 %copy.12 = f32[2,4,32,128]{3,2,1,0:T(8,128)} copy(f32[2,4,32,128]{3,2,1,0:T(8,128)} %bitcast.1) | data formatting | bytes 262144
where the time goes:
time: 46.5 us; the launch traced here: 46.3 us
  Pallas kernels  43.4 us (93%)
  local copies, waits for them, and re-layouts  1.57 us (3%)
  between operations  1.3 us (3%)
    pallas_call x1, Pallas kernels, on_device(): pl.pallas_call(functools.partial(kernel, gz_count, shot_count), out_shape...  43.4 us
    unnamed x1, local copies, waits for them, and re-layouts  1.57 us

commit v1 on v0

v1 whole, which is shorter than its diff:
```python
import functools

import jax
import jax.numpy as jnp
from jax import lax
from jax.experimental import pallas as pl
from jax.experimental.pallas import tpu as pltpu
from jax.sharding import PartitionSpec as P

time_step = 0.15
VX, VY, VZ, SXX, SYY, SZZ, SXY, SXZ, SYZ = range(9)
MESH = pl.DeviceIdType.MESH


def kernel(
    gz_count,
    shot_count,
    wave_hbm,
    earth_hbm,
    src_depth_hbm,
    src_column_hbm,
    wavelet_hbm,
    rec_depth_hbm,
    rec_column_hbm,
    traces_hbm,
    out,
    state,
    earth,
    below,
    below_earth,
    above,
    above_earth,
    first_up,
    first_szz,
    earth_up,
    earth_down,
    low_in,
    high_in,
    up_out,
    down_out,
    rest_in,
    rest_out,
    inject,
    press,
    spin,
    image,
    parts_in,
    own,
    src_depth,
    src_column,
    wavelet,
    rec_depth,
    rec_column,
    traces,
    load_sem,
    init_send,
    init_recv,
    up_send,
    up_recv,
    down_send,
    down_recv,
    rest_sem,
    img_send,
    img_recv,
):
    planes, nx, ny = state.shape[2:]
    steps = traces.shape[0]
    last = planes - 1
    h = time_step
    gz = lax.axis_index("gz")
    shot = lax.axis_index("shot")
    has_low = gz > 0
    has_high = gz < gz_count - 1
    paired = shot_count % 2 == 0
    far = lax.rem(shot, 2) == 0

    def local(src, dst, k):
        return pltpu.make_async_copy(src, dst, load_sem.at[k])

    load_first = [
        [
            local(wave_hbm.at[0, w, pl.ds(SXZ, 2), last], first_up.at[w, pl.ds(0, 2)], 4 * w),
            local(wave_hbm.at[0, w, SZZ, 0], first_szz.at[w], 4 * w + 1),
            local(wave_hbm.at[0, w], state.at[w], 4 * w + 2),
        ]
        for w in range(2)
    ]
    load_edge = [
        local(earth_hbm.at[0, last], earth_up.at[0], 8),
        local(earth_hbm.at[2, last], earth_up.at[1], 9),
        local(earth_hbm.at[:, 0], earth_down, 10),
    ]
    load_earth = local(earth_hbm, earth, 11)
    small = [
        local(src, dst, 12 + i)
        for i, (src, dst) in enumerate(
            (
                (traces_hbm.at[0], traces),
                (rec_depth_hbm, rec_depth),
                (rec_column_hbm, rec_column),
                (src_depth_hbm, src_depth),
                (src_column_hbm, src_column),
                (wavelet_hbm, wavelet),
            )
        )
    ]
    for copy in load_edge[:1] + load_first[0] + load_first[1] + load_edge[1:] + [load_earth] + small:
        copy.start()

    barrier = pltpu.get_barrier_semaphore()

    @pl.when(has_low)
    def _():
        pl.semaphore_signal(barrier, inc=1, device_id={"gz": gz - 1}, device_id_type=MESH)

    @pl.when(has_high)
    def _():
        pl.semaphore_signal(barrier, inc=1, device_id={"gz": gz + 1}, device_id_type=MESH)

    for k in range(1, shot_count):
        peer = lax.rem(shot + k, shot_count)
        pl.semaphore_signal(barrier, inc=1, device_id={"shot": peer}, device_id_type=MESH)

    rows = lax.broadcasted_iota(jnp.int32, (nx, ny), 0)
    lanes = lax.broadcasted_iota(jnp.int32, (nx, ny), 1)
    cells = rows * ny + lanes

    def fx(a):
        return jnp.where(rows == nx - 1, 0.0, pltpu.roll(a, nx - 1, 0)) - a

    def bx(a):
        return a - jnp.where(rows == 0, 0.0, pltpu.roll(a, 1, 0))

    def fy(a):
        return jnp.where(lanes == ny - 1, 0.0, pltpu.roll(a, ny - 1, 1)) - a

    def by(a):
        return a - jnp.where(lanes == 0, 0.0, pltpu.roll(a, 1, 1))

    low_peers = (gz + gz_count - 1) // gz_count
    high_peers = (2 * gz_count - 2 - gz) // gz_count
    pl.semaphore_wait(barrier, low_peers + high_peers + shot_count - 1)

    def remote(src, dst, send, recv, step_to):
        return pltpu.make_async_remote_copy(
            src_ref=src,
            dst_ref=dst,
            send_sem=send,
            recv_sem=recv,
            device_id={"gz": gz + step_to},
            device_id_type=MESH,
        )

    def initial(src, dst, k, step_to):
        return remote(src, dst, init_send.at[k], init_recv.at[k], step_to)

    up_first = [initial(first_up.at[w], below.at[w], w, 1) for w in range(2)]
    up_earth = [initial(earth_up.at[i], below_earth.at[i], 2 + i, 1) for i in range(2)]
    down_first = [initial(first_szz.at[w], above.at[w, 4], 4 + w, -1) for w in range(2)]
    down_near = initial(earth_down.at[0], above_earth.at[0], 6, -1)
    down_far = [
        initial(earth_down, above_earth, 6, -1),
    ] + [
        initial(src, dst, 7 + 3 * w + i, -1)
        for w in range(2)
        for i, (src, dst) in enumerate(
            (
                (wave_hbm.at[0, w, pl.ds(VX, 2), 0], above.at[w, pl.ds(0, 2)]),
                (wave_hbm.at[0, w, pl.ds(SXX, 2), 0], above.at[w, pl.ds(2, 2)]),
                (wave_hbm.at[0, w, SXY, 0], above.at[w, 5]),
            )
        )
    ]

    for w in range(2):
        if w == 0:
            load_edge[0].wait()
        for copy in load_first[w]:
            copy.wait()
        szz, vz = state[w, SZZ, last], state[w, VZ, last]
        first_up[w, 2] = vz + (h * earth_up[0]) * (bx(first_up[w, 0]) + by(first_up[w, 1]) - szz)

        @pl.when(has_high)
        def _(w=w):
            up_first[w].start()
            if w == 0:
                up_earth[0].start()

        @pl.when(has_low)
        def _(w=w):
            down_first[w].start()

    for copy in load_edge[1:]:
        copy.wait()

    @pl.when(has_high)
    def _():
        up_earth[1].start()

    if paired:

        @pl.when(has_low & far)
        def _():
            for copy in down_far:
                copy.start()

        @pl.when(has_low & jnp.logical_not(far))
        def _():
            down_near.start()

    else:

        @pl.when(has_low)
        def _():
            down_near.start()

    @pl.when(jnp.logical_not(has_low))
    def _():
        below[...] = jnp.zeros_like(below)
        below_earth[...] = jnp.zeros_like(below_earth)
        low_in[...] = jnp.zeros_like(low_in)

    @pl.when(jnp.logical_not(has_high))
    def _():
        above[...] = jnp.zeros_like(above)
        above_earth[...] = jnp.zeros_like(above_earth)
        high_in[...] = jnp.zeros_like(high_in)
        rest_in[...] = jnp.zeros_like(rest_in)

    image[...] = jnp.zeros_like(image)
    load_earth.wait()
    earth[...] = earth[...] * h

    for copy in small:
        copy.wait()
    offset = gz * planes
    receivers = traces.shape[1]
    column = rec_column[...]
    depth = rec_depth[...] - offset
    row_ids = lax.broadcasted_iota(jnp.int32, (nx, receivers), 0) * ny
    past = column - row_ids
    on_row = (past >= 0) & (past < ny)
    row_hot = jnp.concatenate(
        [jnp.where(on_row & (depth == p), h, 0.0) for p in range(-1, planes)], axis=0
    )
    col_ids = lax.broadcasted_iota(jnp.int32, (ny, receivers), 0)
    col_hot = jnp.where((column & (ny - 1)) == col_ids, 1.0, 0.0)

    def fill(n, carry):
        inject[n] = lax.dot_general(
            row_hot * traces[pl.ds(n, 1), :],
            col_hot,
            (((1,), (1,)), ((), ())),
            precision=lax.Precision.HIGHEST,
            preferred_element_type=jnp.float32,
        ).reshape(planes + 1, nx, ny)
        return carry

    lax.fori_loop(0, steps, fill, 0)

    src_at = src_depth[0] - offset
    src_cell = src_column[0]

    def source_term(plane, n):
        cell = jnp.where(src_at == plane, src_cell, -1)
        return jnp.where(cells == cell, h * wavelet[0, n], 0.0)

    def parity(n):
        return n % 2 if isinstance(n, int) else lax.rem(n, 2)

    def send_up(w, n):
        return remote(up_out.at[w, n], low_in.at[w, n], up_send.at[w, n], up_recv.at[w, n], 1)

    def send_down(w, n):
        return remote(
            down_out.at[w, n], high_in.at[w, n], down_send.at[w, n], down_recv.at[w, n], -1
        )

    send_rest = remote(rest_out, rest_in, rest_sem.at[0], rest_sem.at[1], -1)

    def strains(w, p, n, vx, vy, dvz, hlam, hmu):
        ex, ey = bx(vx), by(vy)
        spread = hlam * (ex + ey + dvz)
        if w == 0:
            spread = spread + source_term(p, n)
        mu2 = 2.0 * hmu
        return spread + mu2 * ex, spread + mu2 * ey, spread + mu2 * dvz

    def a_node(w, p, n, final=False):
        hb, hlam, hmu = (earth[i, p] for i in range(3))
        sxy = state[w, SXY, p]
        below_p = (below[w, i] for i in range(3)) if p == 0 else (state[w, i, p - 1] for i in (SXZ, SYZ, VZ))
        sxz_b, syz_b, vz_b = below_p
        vx = state[w, VX, p] + hb * (fx(state[w, SXX, p]) + by(sxy) + (state[w, SXZ, p] - sxz_b))
        vy = state[w, VY, p] + hb * (bx(sxy) + fy(state[w, SYY, p]) + (state[w, SYZ, p] - syz_b))
        if w == 1 or not final:
            state[w, VX, p] = vx
            state[w, VY, p] = vy
        dxx, dyy, dzz = strains(w, p, n, vx, vy, state[w, VZ, p] - vz_b, hlam, hmu)
        sxx = state[w, SXX, p] + dxx
        syy = state[w, SYY, p] + dyy
        szz = state[w, SZZ, p] + dzz
        total = sxx + syy + szz
        if not final:
            state[w, SXX, p] = sxx
            state[w, SYY, p] = syy
            state[w, SZZ, p] = szz
        if w == 1 or not final:
            vxy, vyx = fy(vx), fx(vy)
        if not final:
            state[w, SXY, p] = sxy + hmu * (vxy + vyx)
        at = parity(n + 1)
        if w == 0:
            press[at, p] = total * (1.0 / (3 * steps))
        else:
            spin[p] = vyx - vxy
            image[pl.ds(p * nx, nx), :] += press[at, p] * (total * (1.0 / 3.0))
        return vx, vy, szz

    def curl(w, p, n, vxz, vyz, vzx, vzy):
        rotation = (vzy - vyz) + (vxz - vzx) + spin[p]
        image[pl.ds((planes + p) * nx, nx), :] += press[parity(n), p] * rotation

    def b_node(w, p, n, first, upper):
        hb, hmu = earth[0, p], earth[2, p]
        vz, sxz, syz = (state[w, i, p] for i in (VZ, SXZ, SYZ))
        vx_f, vy_f, szz_f = upper
        if not first:
            vxz, vyz = vx_f - state[w, VX, p], vy_f - state[w, VY, p]
            vzx, vzy = fx(vz), fy(vz)
            sxz = sxz + hmu * (vxz + vzx)
            syz = syz + hmu * (vyz + vzy)
            state[w, SXZ, p] = sxz
            state[w, SYZ, p] = syz
            if w == 1:
                curl(w, p, n, vxz, vyz, vzx, vzy)
        term = hb * (bx(sxz) + by(syz) + (szz_f - state[w, SZZ, p]))
        if w == 1:
            term = term + inject[n, p + 1]
        vz = vz + term
        state[w, VZ, p] = vz
        return sxz, syz, vz

    def own_upper(w, p):
        return tuple(state[w, i, p + 1] for i in (VX, VY, SZZ))

    def b_below(w, n, first):
        hb, hmu = below_earth[0], below_earth[1]
        vz = below[w, 2]
        if first:
            term = hb * state[w, SZZ, 0]
        else:
            vx_m, vy_m, szz_m = (low_in[w, n - 1, i] for i in range(3))
            sxz = below[w, 0] + hmu * ((state[w, VX, 0] - vx_m) + fx(vz))
            syz = below[w, 1] + hmu * ((state[w, VY, 0] - vy_m) + fy(vz))
            below[w, 0] = sxz
            below[w, 1] = syz
            term = hb * (bx(sxz) + by(syz) + (state[w, SZZ, 0] - szz_m))
        if w == 1:
            term = term + inject[n, 0]
        below[w, 2] = vz + term

    def above_velocity(w, sxz, syz):
        hb = above_earth[0]
        sxx, syy, sxy = above[w, 2], above[w, 3], above[w, 5]
        vx = above[w, 0] + hb * (fx(sxx) + by(sxy) + (sxz - state[w, SXZ, last]))
        vy = above[w, 1] + hb * (bx(sxy) + fy(syy) + (syz - state[w, SYZ, last]))
        return vx, vy

    def a_above(w, n):
        sxz, syz, vz = (high_in[w, n - 1, i] for i in range(3))
        hlam, hmu = above_earth[1], above_earth[2]
        vx, vy = above_velocity(w, sxz, syz)
        above[w, 0] = vx
        above[w, 1] = vy
        dxx, dyy, dzz = strains(w, planes, n - 1, vx, vy, vz - state[w, VZ, last], hlam, hmu)
        szz = above[w, 4] + dzz
        above[w, 2] += dxx
        above[w, 3] += dyy
        above[w, 4] = szz
        above[w, 5] += hmu * (fy(vx) + fx(vy))
        return vx, vy, szz

    inner = range(1, last)

    def run(deep):
        def inside(w, n):
            for p in range(1 if deep else 0, last):
                b_node(w, p, n, isinstance(n, int) and n == 0, own_upper(w, p))
            for p in inner:
                a_node(w, p, n)

        def store(buf, values, w, n):
            for i, value in enumerate(values):
                buf[w, n, i] = value

        def lowest_down(w, n):
            values = b_node(w, 0, n, isinstance(n, int) and n == 0, own_upper(w, 0))
            store(down_out, values, w, n)
            wanted = has_low if w == 1 else has_low & (n < steps - 1)

            @pl.when(wanted)
            def _():
                send_down(w, n).start()

        def half(w, n, first, final):
            if first:

                @pl.when(has_high)
                def _():
                    down_first[w].wait_recv()

            else:

                @pl.when(has_high)
                def _():
                    send_down(w, n - 1).wait_recv()

            def wait_low():
                @pl.when(has_low)
                def _():
                    if first:
                        up_first[w].wait_recv()
                        if w == 0:
                            up_earth[0].wait_recv()
                    else:
                        send_up(w, n - 1).wait_recv()

                if first and w == 0:
                    below_earth[0] = below_earth[0] * h

            if not deep:
                wait_low()
            if first:
                upper = (None, None, above[w, 4])
            elif deep:
                upper = a_above(w, n)
            else:
                upper = tuple(high_in[w, n - 1, i] for i in range(3))
            if deep:
                b_node(w, last, n, first, upper)
                values = a_node(w, last, n, final)
                if not final:
                    store(up_out, values, w, n)

                    @pl.when(has_high)
                    def _():
                        send_up(w, n).start()

                wait_low()
                b_below(w, n, first)
                a_node(w, 0, n, final)
                if not final:
                    lowest_down(w, n + 1)
            else:
                b_below(w, n, first)
                b_node(w, last, n, first, upper)
                lower = a_node(w, 0, n, final)
                values = a_node(w, last, n, final)
                if not final:
                    store(down_out, lower, w, n)
                    store(up_out, values, w, n)

                    @pl.when(has_low)
                    def _():
                        send_down(w, n).start()

                    @pl.when(has_high)
                    def _():
                        send_up(w, n).start()

            if not final:
                inside(w, n + 1)
                if w == 1 and not deep:

                    @pl.when(has_low & (n == steps - 2))
                    def _():
                        hb, sxy = earth[0, 0], state[1, SXY, 0]
                        rest_out[0] = state[1, VX, 0] + hb * (
                            fx(state[1, SXX, 0]) + by(sxy) + state[1, SXZ, 0]
                        )
                        rest_out[1] = state[1, VY, 0] + hb * (
                            bx(sxy) + fy(state[1, SYY, 0]) + state[1, SYZ, 0]
                        )
                        send_rest.start()

            elif w == 1:

                @pl.when(has_high)
                def _():
                    if deep:
                        send_down(1, n).wait_recv()
                    else:
                        send_rest.wait_recv()

                if deep:
                    vx_p, vy_p = above_velocity(1, high_in[1, n, 0], high_in[1, n, 1])
                else:
                    hb = above_earth[0]
                    vx_p = rest_in[0] - hb * state[1, SXZ, last]
                    vy_p = rest_in[1] - hb * state[1, SYZ, last]
                for p in range(planes):
                    vx_f = vx_p if p == last else state[1, VX, p + 1]
                    vy_f = vy_p if p == last else state[1, VY, p + 1]
                    vz = state[1, VZ, p]
                    curl(1, p, n + 1, vx_f - state[1, VX, p], vy_f - state[1, VY, p], fx(vz), fy(vz))

        for w in range(2):
            if deep:
                lowest_down(w, 0)
            inside(w, 0)
        for w in range(2):
            half(w, 0, True, False)

        @pl.when(has_low)
        def _():
            up_earth[1].wait_recv()

        below_earth[1] = below_earth[1] * h

        @pl.when(has_high)
        def _():
            for copy in down_far if deep else [down_near]:
                copy.wait_recv()

        for i in range(3 if deep else 1):
            above_earth[i] = above_earth[i] * h

        def body(n, carry):
            for w in range(2):
                half(w, n, False, False)
            return carry

        lax.fori_loop(1, steps - 1, body, 0)
        for w in range(2):
            half(w, steps - 1, False, True)

    if paired:
        pl.when(far)(lambda: run(True))
        pl.when(jnp.logical_not(far))(lambda: run(False))
    else:
        run(False)

    total = image.shape[0]
    chunk = total // shot_count

    def span(index):
        return pl.ds(pl.multiple_of(index * chunk, 8), chunk)

    scatter = []
    for k in range(1, shot_count):
        peer = lax.rem(shot + k, shot_count)
        copy = pltpu.make_async_remote_copy(
            src_ref=image.at[span(peer)],
            dst_ref=parts_in.at[k - 1],
            send_sem=img_send.at[0, k - 1],
            recv_sem=img_recv.at[0, k - 1],
            device_id={"shot": peer},
            device_id_type=MESH,
        )
        copy.start()
        scatter.append(copy)
    acc = image[span(shot), :]
    for k in range(1, shot_count):
        scatter[k - 1].wait_recv()
        acc = acc + parts_in[k - 1]
    own[...] = acc
    gather = []
    for k in range(1, shot_count):
        peer = lax.rem(shot + k, shot_count)
        copy = pltpu.make_async_remote_copy(
            src_ref=own,
            dst_ref=out.at[span(shot)],
            send_sem=img_send.at[1, k - 1],
            recv_sem=img_recv.at[1, k - 1],
            device_id={"shot": peer},
            device_id_type=MESH,
        )
        copy.start()
        gather.append(copy)
    out[span(shot), :] = acc

    @pl.when(has_high)
    def _():
        for copy in up_first + up_earth:
            copy.wait_send()

    @pl.when(has_low)
    def _():
        for copy in down_first:
            copy.wait_send()

    def drain_near():
        @pl.when(has_low)
        def _():
            down_near.wait_send()
            send_rest.wait_send()

    def drain_far():
        @pl.when(has_low)
        def _():
            for copy in down_far:
                copy.wait_send()
            send_down(1, steps - 1).wait_send()

    if paired:
        pl.when(far)(drain_far)
        pl.when(jnp.logical_not(far))(drain_near)
    else:
        drain_near()

    def drain(n, carry):
        for w in range(2):

            @pl.when(has_high)
            def _(w=w):
                send_up(w, n).wait_send()

            @pl.when(has_low)
            def _(w=w):
                send_down(w, n).wait_send()

        return carry

    lax.fori_loop(0, steps - 1, drain, 0)
    for copy in scatter:
        copy.wait_send()
    for copy in gather:
        copy.wait()


def on_device(
    gz_count,
    shot_count,
    wavefields,
    earth_model,
    source_depth,
    source_column,
    wavelet,
    receiver_depth,
    receiver_column,
    traces,
):
    planes, nx, ny = wavefields.shape[3:]
    steps = wavelet.shape[1]
    rows = 2 * planes * nx
    peers = max(shot_count - 1, 1)
    f32 = jnp.float32
    vmem = pl.BlockSpec(memory_space=pltpu.VMEM)
    hbm = pl.BlockSpec(memory_space=pltpu.HBM)
    dma = pltpu.SemaphoreType.DMA

    def plane(*lead):
        return pltpu.VMEM((*lead, nx, ny), f32)

    summed = pl.pallas_call(
        functools.partial(kernel, gz_count, shot_count),
        out_shape=jax.ShapeDtypeStruct((rows, ny), f32),
        in_specs=[hbm] * 8,
        out_specs=vmem,
        scratch_shapes=[
            plane(2, 9, planes),
            plane(3, planes),
            plane(2, 3),
            plane(2),
            plane(2, 6),
            plane(3),
            plane(2, 3),
            plane(2),
            plane(2),
            plane(3),
            plane(2, steps, 3),
            plane(2, steps, 3),
            plane(2, steps, 3),
            plane(2, steps, 3),
            plane(2),
            plane(2),
            plane(steps, planes + 1),
            plane(2, planes),
            plane(planes),
            pltpu.VMEM((rows, ny), f32),
            pltpu.VMEM((peers, rows // shot_count, ny), f32),
            pltpu.VMEM((rows // shot_count, ny), f32),
            pltpu.SMEM(source_depth.shape, jnp.int32),
            pltpu.SMEM(source_column.shape, jnp.int32),
            pltpu.SMEM(wavelet.shape, f32),
            pltpu.VMEM(receiver_depth.shape, jnp.int32),
            pltpu.VMEM(receiver_column.shape, jnp.int32),
            pltpu.VMEM(traces.shape[1:], f32),
            dma((18,)),
            dma((13,)),
            dma((13,)),
            dma((2, steps)),
            dma((2, steps)),
            dma((2, steps)),
            dma((2, steps)),
            dma((2,)),
            dma((2, peers)),
            dma((2, peers)),
        ],
        compiler_params=pltpu.CompilerParams(collective_id=0, has_side_effects=True),
    )(
        wavefields,
        earth_model,
        source_depth,
        source_column,
        wavelet,
        receiver_depth,
        receiver_column,
        traces,
    )
    return summed.reshape(2, planes, nx, ny)


def solution(mesh):
    placed = (
        P(("parts", "shot"), None, None, "gz", None, None),
        P("parts", "gz", None, None),
        P(("parts", "shot")),
        P(("parts", "shot")),
        P(("parts", "shot"), None),
        P(("parts", "shot"), None),
        P(("parts", "shot"), None),
        P(("parts", "shot"), None, None),
    )
    return jax.shard_map(
        functools.partial(on_device, mesh.shape["gz"], mesh.shape["shot"]),
        mesh=mesh,
        in_specs=placed,
        out_specs=P("parts", "gz", None, None),
        check_vma=False,
    )
```

time: 46.5 us -> 39 us (0.84)
  Pallas kernels: 43.4 us -> 35.9 us
    pallas_call x1, Pallas kernels: 43.4 us -> 35.9 us  [on_device(): pl.pallas_call(functools.partial(kernel, gz_count, shot_count), out_shape...]
where the time goes in v1:
time: 39 us; the launch traced here: 38.8 us
  Pallas kernels  35.9 us (92%)
  local copies, waits for them, and re-layouts  1.57 us (4%)
  between operations  1.3 us (3%)
    pallas_call x1, Pallas kernels, on_device(): pl.pallas_call(functools.partial(kernel, gz_count, shot_count), out_shape...  35.9 us
    unnamed x1, local copies, waits for them, and re-layouts  1.57 us

profile of v1, /device:TPU:0, one launch (start us, length us, event | category | flops | bytes accessed | tf_op | source)
XLA Modules:
  0.0 38.8 jit_solution(13003505379720249111)
XLA Ops:
  1.3 35.9 %shard_map.82 = f32[256,128]{1,0:T(8,128)} custom-call(f32[1,2,9,4,32,128]{5,4,3,2,1,0:T(8,128)} %wave_hbm.1, f32[3,4,32,128]{3,2,1,0:T(8,128)} %earth_hbm.1, s32[1]{0:T(128)S(6)} %copy.10.src_depth_hbm, s32[1]{0:T(128)S(6)} %copy.11.src_column_hbm, f32[1,8]{1,0:T(1,128)} %wavelet_hbm.1, s32[1,64]{1,0:T(1,128)} %rec_depth_hbm.1, s32[1,64]{1,0:T(1,128)} %rec_column_hbm.1, ...), custom_call_target="tpu_custom_call" | custom-call | tf_op jit(solution)/shard_map/pallas_call | solution.py:656
  37.2 1.6 %copy.12 = f32[2,4,32,128]{3,2,1,0:T(8,128)} copy(f32[2,4,32,128]{3,2,1,0:T(8,128)} %bitcast.1) | data formatting | bytes 262144

commit v2 on v1

--- a/solution.py
+++ b/solution.py
@@ -43,6 +43,10 @@
     inject,
     press,
     spin,
+    slope,
+    grad,
+    strain,
+    twist,
     image,
     parts_in,
     own,
@@ -286,36 +290,35 @@
         mu2 = 2.0 * hmu
         return spread + mu2 * ex, spread + mu2 * ey, spread + mu2 * dvz
 
-    def a_node(w, p, n, final=False):
+    def keep_pressure(w, p, n, total):
+        at = parity(n + 1)
+        if w == 0:
+            press[at, p] = total * (1.0 / (3 * steps))
+        else:
+            image[pl.ds(p * nx, nx), :] += press[at, p] * (total * (1.0 / 3.0))
+
+    def a_node(w, p, n):
         hb, hlam, hmu = (earth[i, p] for i in range(3))
         sxy = state[w, SXY, p]
         below_p = (below[w, i] for i in range(3)) if p == 0 else (state[w, i, p - 1] for i in (SXZ, SYZ, VZ))
         sxz_b, syz_b, vz_b = below_p
         vx = state[w, VX, p] + hb * (fx(state[w, SXX, p]) + by(sxy) + (state[w, SXZ, p] - sxz_b))
         vy = state[w, VY, p] + hb * (bx(sxy) + fy(state[w, SYY, p]) + (state[w, SYZ, p] - syz_b))
-        if w == 1 or not final:
-            state[w, VX, p] = vx
-            state[w, VY, p] = vy
+        state[w, VX, p] = vx
+        state[w, VY, p] = vy
         dxx, dyy, dzz = strains(w, p, n, vx, vy, state[w, VZ, p] - vz_b, hlam, hmu)
         sxx = state[w, SXX, p] + dxx
         syy = state[w, SYY, p] + dyy
         szz = state[w, SZZ, p] + dzz
         total = sxx + syy + szz
-        if not final:
-            state[w, SXX, p] = sxx
-            state[w, SYY, p] = syy
-            state[w, SZZ, p] = szz
-        if w == 1 or not final:
-            vxy, vyx = fy(vx), fx(vy)
-        if not final:
-            state[w, SXY, p] = sxy + hmu * (vxy + vyx)
-        at = parity(n + 1)
-        if w == 0:
-            press[at, p] = total * (1.0 / (3 * steps))
-        else:
+        state[w, SXX, p] = sxx
+        state[w, SYY, p] = syy
+        state[w, SZZ, p] = szz
+        vxy, vyx = fy(vx), fx(vy)
+        state[w, SXY, p] = sxy + hmu * (vxy + vyx)
+        keep_pressure(w, p, n, total)
+        if w == 1:
             spin[p] = vyx - vxy
-            image[pl.ds(p * nx, nx), :] += press[at, p] * (total * (1.0 / 3.0))
-        return vx, vy, szz
 
     def curl(w, p, n, vxz, vyz, vzx, vzy):
         rotation = (vzy - vyz) + (vxz - vzx) + spin[p]
@@ -344,6 +347,108 @@
     def own_upper(w, p):
         return tuple(state[w, i, p + 1] for i in (VX, VY, SZZ))
 
+    BELOW, LAST, LOWEST = range(3)
+    ABOVE = 2
+
+    def edge_at(p):
+        return 0 if p == 0 else 1
+
+    def set_slope(w, slot, vz):
+        slope[w, slot, 0] = fx(vz)
+        slope[w, slot, 1] = fy(vz)
+
+    def set_grad(w, slot, sxx, syy, sxy):
+        grad[w, slot, 0] = fx(sxx) + by(sxy)
+        grad[w, slot, 1] = bx(sxy) + fy(syy)
+
+    def edge_velocity(w, p):
+        hb = earth[0, p]
+        if p == 0:
+            sxz_b, syz_b = below[w, 0], below[w, 1]
+        else:
+            sxz_b, syz_b = state[w, SXZ, p - 1], state[w, SYZ, p - 1]
+        at = edge_at(p)
+        vx = state[w, VX, p] + hb * (grad[w, at, 0] + (state[w, SXZ, p] - sxz_b))
+        vy = state[w, VY, p] + hb * (grad[w, at, 1] + (state[w, SYZ, p] - syz_b))
+        dvz = state[w, VZ, p] - (below[w, 2] if p == 0 else state[w, VZ, p - 1])
+        return vx, vy, dvz
+
+    def widen(w, at, p, n, vx, vy, dvz, hlam, hmu, szz):
+        ey = by(vy)
+        spread = hlam * (bx(vx) + ey + dvz)
+        if w == 0:
+            spread = spread + source_term(p, n)
+        strain[w, at, 0] = spread
+        strain[w, at, 1] = ey
+        return szz + (spread + (2.0 * hmu) * dvz)
+
+    def a_fast(w, p, n):
+        vx, vy, dvz = edge_velocity(w, p)
+        state[w, VX, p] = vx
+        state[w, VY, p] = vy
+        szz = widen(w, edge_at(p), p, n, vx, vy, dvz, earth[1, p], earth[2, p], state[w, SZZ, p])
+        state[w, SZZ, p] = szz
+        return vx, vy, szz
+
+    def rest_of(w, at, vx, vy, hmu, sxx, syy, sxy):
+        spread, mu2 = strain[w, at, 0], 2.0 * hmu
+        vxy, vyx = fy(vx), fx(vy)
+        sxx = sxx + (spread + mu2 * bx(vx))
+        syy = syy + (spread + mu2 * strain[w, at, 1])
+        sxy = sxy + hmu * (vxy + vyx)
+        set_grad(w, at, sxx, syy, sxy)
+        return sxx, syy, sxy, vyx - vxy
+
+    def a_slow(w, p, n):
+        sxx, syy, sxy, turn = rest_of(
+            w, edge_at(p), *(state[w, i, p] for i in (VX, VY)), earth[2, p],
+            *(state[w, i, p] for i in (SXX, SYY, SXY)),
+        )
+        state[w, SXX, p] = sxx
+        state[w, SYY, p] = syy
+        state[w, SXY, p] = sxy
+        keep_pressure(w, p, n, sxx + syy + state[w, SZZ, p])
+        if w == 1:
+            spin[p] = turn
+
+    def a_final(w, p, n):
+        vx, vy, dvz = edge_velocity(w, p)
+        volume = bx(vx) + by(vy) + dvz
+        spread = earth[1, p] * volume
+        if w == 0:
+            spread = spread + source_term(p, n)
+        total = state[w, SXX, p] + state[w, SYY, p] + state[w, SZZ, p]
+        keep_pressure(w, p, n, total + (3.0 * spread + (2.0 * earth[2, p]) * volume))
+        if w == 1:
+            state[1, VX, p] = vx
+            state[1, VY, p] = vy
+            spin[p] = fx(vy) - fy(vx)
+
+    def b_fast(w, p, slot, n, first, upper):
+        hb, hmu = earth[0, p], earth[2, p]
+        vz, sxz, syz = (state[w, i, p] for i in (VZ, SXZ, SYZ))
+        vx_f, vy_f, szz_f = upper
+        if not first:
+            vxz, vyz = vx_f - state[w, VX, p], vy_f - state[w, VY, p]
+            vzx, vzy = slope[w, slot, 0], slope[w, slot, 1]
+            sxz = sxz + hmu * (vxz + vzx)
+            syz = syz + hmu * (vyz + vzy)
+            state[w, SXZ, p] = sxz
+            state[w, SYZ, p] = syz
+            if w == 1:
+                twist[edge_at(p)] = (vzy - vyz) + (vxz - vzx)
+        term = hb * (bx(sxz) + by(syz) + (szz_f - state[w, SZZ, p]))
+        if w == 1:
+            term = term + inject[n, p + 1]
+        vz = vz + term
+        state[w, VZ, p] = vz
+        return sxz, syz, vz
+
+    def keep_twist(p, n):
+        image[pl.ds((planes + p) * nx, nx), :] += press[parity(n), p] * (
+            twist[edge_at(p)] + spin[p]
+        )
+
     def b_below(w, n, first):
         hb, hmu = below_earth[0], below_earth[1]
         vz = below[w, 2]
@@ -351,8 +456,8 @@
             term = hb * state[w, SZZ, 0]
         else:
             vx_m, vy_m, szz_m = (low_in[w, n - 1, i] for i in range(3))
-            sxz = below[w, 0] + hmu * ((state[w, VX, 0] - vx_m) + fx(vz))
-            syz = below[w, 1] + hmu * ((state[w, VY, 0] - vy_m) + fy(vz))
+            sxz = below[w, 0] + hmu * ((state[w, VX, 0] - vx_m) + slope[w, BELOW, 0])
+            syz = below[w, 1] + hmu * ((state[w, VY, 0] - vy_m) + slope[w, BELOW, 1])
             below[w, 0] = sxz
             below[w, 1] = syz
             term = hb * (bx(sxz) + by(syz) + (state[w, SZZ, 0] - szz_m))
@@ -362,24 +467,27 @@
 
     def above_velocity(w, sxz, syz):
         hb = above_earth[0]
-        sxx, syy, sxy = above[w, 2], above[w, 3], above[w, 5]
-        vx = above[w, 0] + hb * (fx(sxx) + by(sxy) + (sxz - state[w, SXZ, last]))
-        vy = above[w, 1] + hb * (bx(sxy) + fy(syy) + (syz - state[w, SYZ, last]))
+        vx = above[w, 0] + hb * (grad[w, ABOVE, 0] + (sxz - state[w, SXZ, last]))
+        vy = above[w, 1] + hb * (grad[w, ABOVE, 1] + (syz - state[w, SYZ, last]))
         return vx, vy
 
-    def a_above(w, n):
+    def above_fast(w, n):
         sxz, syz, vz = (high_in[w, n - 1, i] for i in range(3))
-        hlam, hmu = above_earth[1], above_earth[2]
         vx, vy = above_velocity(w, sxz, syz)
         above[w, 0] = vx
         above[w, 1] = vy
-        dxx, dyy, dzz = strains(w, planes, n - 1, vx, vy, vz - state[w, VZ, last], hlam, hmu)
-        szz = above[w, 4] + dzz
-        above[w, 2] += dxx
-        above[w, 3] += dyy
+        dvz = vz - state[w, VZ, last]
+        szz = widen(w, ABOVE, planes, n - 1, vx, vy, dvz, above_earth[1], above_earth[2], above[w, 4])
         above[w, 4] = szz
-        above[w, 5] += hmu * (fy(vx) + fx(vy))
         return vx, vy, szz
+
+    def above_slow(w):
+        sxx, syy, sxy, _ = rest_of(
+            w, ABOVE, above[w, 0], above[w, 1], above_earth[2], above[w, 2], above[w, 3], above[w, 5]
+        )
+        above[w, 2] = sxx
+        above[w, 3] = syy
+        above[w, 5] = sxy
 
     inner = range(1, last)
 
@@ -395,7 +503,7 @@
                 buf[w, n, i] = value
 
         def lowest_down(w, n):
-            values = b_node(w, 0, n, isinstance(n, int) and n == 0, own_upper(w, 0))
+            values = b_fast(w, 0, LOWEST, n, isinstance(n, int) and n == 0, own_upper(w, 0))
             store(down_out, values, w, n)
             wanted = has_low if w == 1 else has_low & (n < steps - 1)
 
@@ -434,54 +542,67 @@
             if first:
                 upper = (None, None, above[w, 4])
             elif deep:
-                upper = a_above(w, n)
+                upper = above_fast(w, n)
             else:
                 upper = tuple(high_in[w, n - 1, i] for i in range(3))
-            if deep:
-                b_node(w, last, n, first, upper)
-                values = a_node(w, last, n, final)
-                if not final:
-                    store(up_out, values, w, n)
-
-                    @pl.when(has_high)
-                    def _():
-                        send_up(w, n).start()
+            if final:
+                if deep:
+                    wait_low()
+                b_fast(w, last, LAST, n, first, upper)
+                b_below(w, n, first)
+                if w == 1:
+                    keep_twist(last, n)
+                    if deep:
+                        above_slow(w)
+                a_final(w, 0, n)
+                a_final(w, last, n)
+            elif deep:
+                b_fast(w, last, LAST, n, first, upper)
+                store(up_out, a_fast(w, last, n), w, n)
+
+                @pl.when(has_high)
+                def _():
+                    send_up(w, n).start()
 
                 wait_low()
                 b_below(w, n, first)
-                a_node(w, 0, n, final)
-                if not final:
-                    lowest_down(w, n + 1)
+                a_fast(w, 0, n)
+                lowest_down(w, n + 1)
             else:
                 b_below(w, n, first)
-                b_node(w, last, n, first, upper)
-                lower = a_node(w, 0, n, final)
-                values = a_node(w, last, n, final)
-                if not final:
-                    store(down_out, lower, w, n)
-                    store(up_out, values, w, n)
-
-                    @pl.when(has_low)
-                    def _():
-                        send_down(w, n).start()
-
-                    @pl.when(has_high)
-                    def _():
-                        send_up(w, n).start()
+                b_fast(w, last, LAST, n, first, upper)
+                store(down_out, a_fast(w, 0, n), w, n)
+                store(up_out, a_fast(w, last, n), w, n)
+
+                @pl.when(has_low)
+                def _():
+                    send_down(w, n).start()
+
+                @pl.when(has_high)
+                def _():
+                    send_up(w, n).start()
 
             if not final:
+                if w == 1 and not first:
+                    keep_twist(last, n)
+                a_slow(w, 0, n)
+                a_slow(w, last, n)
+                if deep:
+                    if not first:
+                        above_slow(w)
+                    if w == 1:
+                        keep_twist(0, n + 1)
+                    set_slope(w, LOWEST, state[w, VZ, 0])
+                set_slope(w, BELOW, below[w, 2])
+                set_slope(w, LAST, state[w, VZ, last])
                 inside(w, n + 1)
                 if w == 1 and not deep:
 
                     @pl.when(has_low & (n == steps - 2))
                     def _():
-                        hb, sxy = earth[0, 0], state[1, SXY, 0]
-                        rest_out[0] = state[1, VX, 0] + hb * (
-                            fx(state[1, SXX, 0]) + by(sxy) + state[1, SXZ, 0]
-                        )
-                        rest_out[1] = state[1, VY, 0] + hb * (
-                            bx(sxy) + fy(state[1, SYY, 0]) + state[1, SYZ, 0]
-                        )
+                        hb = earth[0, 0]
+                        rest_out[0] = state[1, VX, 0] + hb * (grad[1, 0, 0] + state[1, SXZ, 0])
+                        rest_out[1] = state[1, VY, 0] + hb * (grad[1, 0, 1] + state[1, SYZ, 0])
                         send_rest.start()
 
             elif w == 1:
@@ -508,6 +629,9 @@
         for w in range(2):
             if deep:
                 lowest_down(w, 0)
+                set_slope(w, LOWEST, state[w, VZ, 0])
+            for p in sorted({0, last}):
+                set_grad(w, edge_at(p), *(state[w, i, p] for i in (SXX, SYY, SXY)))
             inside(w, 0)
         for w in range(2):
             half(w, 0, True, False)
@@ -525,6 +649,9 @@
 
         for i in range(3 if deep else 1):
             above_earth[i] = above_earth[i] * h
+        if deep:
+            for w in range(2):
+                set_grad(w, ABOVE, above[w, 2], above[w, 3], above[w, 5])
 
         def body(n, carry):
             for w in range(2):
@@ -655,7 +782,7 @@
 
     summed = pl.pallas_call(
         functools.partial(kernel, gz_count, shot_count),
-        out_shape=jax.ShapeDtypeStruct((rows, ny), f32),
+        out_shape=pltpu.VMEM((rows, ny), f32),
         in_specs=[hbm] * 8,
         out_specs=vmem,
         scratch_shapes=[
@@ -678,6 +805,10 @@
             plane(steps, planes + 1),
             plane(2, planes),
             plane(planes),
+            plane(2, 3, 2),
+            plane(2, 3, 2),
+            plane(2, 3, 2),
+            plane(2),
             pltpu.VMEM((rows, ny), f32),
             pltpu.VMEM((peers, rows // shot_count, ny), f32),
             pltpu.VMEM((rows // shot_count, ny), f32),

time: 39 us -> 36.9 us (0.946)
  Pallas kernels: 35.9 us -> 34.8 us
  local copies, waits for them, and re-layouts: 1.57 us -> 0.66 us
    pallas_call x1, Pallas kernels: 35.9 us -> 34.8 us  [on_device(): pl.pallas_call(functools.partial(kernel, gz_count, shot_count), out_shape...]
    unnamed x1, local copies, waits for them, and re-layouts: 1.57 us -> 0.66 us
where the time goes in v2:
time: 36.9 us; the launch traced here: 36.7 us
  Pallas kernels  34.8 us (94%)
  between operations  1.3 us (4%)
  local copies, waits for them, and re-layouts  0.66 us (2%)
    pallas_call x1, Pallas kernels, on_device(): pl.pallas_call(functools.partial(kernel, gz_count, shot_count), out_shape...  34.8 us

profile of v2, /device:TPU:0, one launch (start us, length us, event | category | flops | bytes accessed | tf_op | source)
XLA Modules:
  0.0 36.7 jit_solution(965194824218303930)
XLA Ops:
  1.3 34.8 %shard_map.82 = f32[256,128]{1,0:T(8,128)S(1)} custom-call(f32[1,2,9,4,32,128]{5,4,3,2,1,0:T(8,128)} %wave_hbm.1, f32[3,4,32,128]{3,2,1,0:T(8,128)} %earth_hbm.1, s32[1]{0:T(128)S(6)} %copy.11.src_depth_hbm, s32[1]{0:T(128)S(6)} %copy.12.src_column_hbm, f32[1,8]{1,0:T(1,128)} %wavelet_hbm.1, s32[1,64]{1,0:T(1,128)} %rec_depth_hbm.1, s32[1,64]{1,0:T(1,128)} %rec_column_hbm.1, ...), custom_call_target="tpu_custom_call" | custom-call | tf_op jit(solution)/shard_map/pallas_call | solution.py:783
  36.1 0.7 %copy.10 = f32[2,4,32,128]{3,2,1,0:T(8,128)} copy(f32[2,4,32,128]{3,2,1,0:T(8,128)S(1)} %bitcast.1) | data formatting | bytes 262144

commit v3 on v2

--- a/solution.py
+++ b/solution.py
@@ -48,8 +48,9 @@
     strain,
     twist,
     image,
-    parts_in,
-    own,
+    near_in,
+    near_sum,
+    cross_in,
     src_depth,
     src_column,
     wavelet,
@@ -64,8 +65,10 @@
     down_send,
     down_recv,
     rest_sem,
-    img_send,
-    img_recv,
+    near_send,
+    near_recv,
+    cross_send,
+    cross_recv,
 ):
     planes, nx, ny = state.shape[2:]
     steps = traces.shape[0]
@@ -272,12 +275,25 @@
     def parity(n):
         return n % 2 if isinstance(n, int) else lax.rem(n, 2)
 
-    def send_up(w, n):
-        return remote(up_out.at[w, n], low_in.at[w, n], up_send.at[w, n], up_recv.at[w, n], 1)
-
-    def send_down(w, n):
+    def part_of(ref, w, n, part):
+        return ref.at[w, n, pl.ds(0, 2)] if part == 0 else ref.at[w, n, 2]
+
+    def send_up(w, n, part):
         return remote(
-            down_out.at[w, n], high_in.at[w, n], down_send.at[w, n], down_recv.at[w, n], -1
+            part_of(up_out, w, n, part),
+            part_of(low_in, w, n, part),
+            up_send.at[w, n, part],
+            up_recv.at[w, n, part],
+            1,
+        )
+
+    def send_down(w, n, part):
+        return remote(
+            part_of(down_out, w, n, part),
+            part_of(high_in, w, n, part),
+            down_send.at[w, n, part],
+            down_recv.at[w, n, part],
+            -1,
         )
 
     send_rest = remote(rest_out, rest_in, rest_sem.at[0], rest_sem.at[1], -1)
@@ -370,25 +386,37 @@
         at = edge_at(p)
         vx = state[w, VX, p] + hb * (grad[w, at, 0] + (state[w, SXZ, p] - sxz_b))
         vy = state[w, VY, p] + hb * (grad[w, at, 1] + (state[w, SYZ, p] - syz_b))
-        dvz = state[w, VZ, p] - (below[w, 2] if p == 0 else state[w, VZ, p - 1])
-        return vx, vy, dvz
-
-    def widen(w, at, p, n, vx, vy, dvz, hlam, hmu, szz):
+        return vx, vy
+
+    def edge_rise(w, p):
+        return state[w, VZ, p] - (below[w, 2] if p == 0 else state[w, VZ, p - 1])
+
+    def widen(w, at, p, n, vx, vy, hlam, hmu):
         ey = by(vy)
-        spread = hlam * (bx(vx) + ey + dvz)
-        if w == 0:
-            spread = spread + source_term(p, n)
-        strain[w, at, 0] = spread
         strain[w, at, 1] = ey
-        return szz + (spread + (2.0 * hmu) * dvz)
+        flat = bx(vx) + ey
+
+        def finish(dvz):
+            spread = hlam * (flat + dvz)
+            if w == 0:
+                spread = spread + source_term(p, n)
+            strain[w, at, 0] = spread
+            return spread + (2.0 * hmu) * dvz
+
+        return finish
 
     def a_fast(w, p, n):
-        vx, vy, dvz = edge_velocity(w, p)
+        vx, vy = edge_velocity(w, p)
         state[w, VX, p] = vx
         state[w, VY, p] = vy
-        szz = widen(w, edge_at(p), p, n, vx, vy, dvz, earth[1, p], earth[2, p], state[w, SZZ, p])
-        state[w, SZZ, p] = szz
-        return vx, vy, szz
+        change = widen(w, edge_at(p), p, n, vx, vy, earth[1, p], earth[2, p])
+
+        def finish():
+            szz = state[w, SZZ, p] + change(edge_rise(w, p))
+            state[w, SZZ, p] = szz
+            return szz
+
+        return (vx, vy), finish
 
     def rest_of(w, at, vx, vy, hmu, sxx, syy, sxy):
         spread, mu2 = strain[w, at, 0], 2.0 * hmu
@@ -412,8 +440,8 @@
             spin[p] = turn
 
     def a_final(w, p, n):
-        vx, vy, dvz = edge_velocity(w, p)
-        volume = bx(vx) + by(vy) + dvz
+        vx, vy = edge_velocity(w, p)
+        volume = bx(vx) + by(vy) + edge_rise(w, p)
         spread = earth[1, p] * volume
         if w == 0:
             spread = spread + source_term(p, n)
@@ -424,11 +452,10 @@
             state[1, VY, p] = vy
             spin[p] = fx(vy) - fy(vx)
 
-    def b_fast(w, p, slot, n, first, upper):
-        hb, hmu = earth[0, p], earth[2, p]
-        vz, sxz, syz = (state[w, i, p] for i in (VZ, SXZ, SYZ))
-        vx_f, vy_f, szz_f = upper
+    def b_fast(w, p, slot, n, first, vx_f, vy_f):
+        sxz, syz = state[w, SXZ, p], state[w, SYZ, p]
         if not first:
+            hmu = earth[2, p]
             vxz, vyz = vx_f - state[w, VX, p], vy_f - state[w, VY, p]
             vzx, vzy = slope[w, slot, 0], slope[w, slot, 1]
             sxz = sxz + hmu * (vxz + vzx)
@@ -437,12 +464,19 @@
             state[w, SYZ, p] = syz
             if w == 1:
                 twist[edge_at(p)] = (vzy - vyz) + (vxz - vzx)
-        term = hb * (bx(sxz) + by(syz) + (szz_f - state[w, SZZ, p]))
-        if w == 1:
-            term = term + inject[n, p + 1]
-        vz = vz + term
-        state[w, VZ, p] = vz
-        return sxz, syz, vz
+
+        def flat():
+            return bx(sxz) + by(syz)
+
+        def finish(shear, szz_f):
+            term = earth[0, p] * (shear + (szz_f - state[w, SZZ, p]))
+            if w == 1:
+                term = term + inject[n, p + 1]
+            vz = state[w, VZ, p] + term
+            state[w, VZ, p] = vz
+            return vz
+
+        return (sxz, syz), flat, finish
 
     def keep_twist(p, n):
         image[pl.ds((planes + p) * nx, nx), :] += press[parity(n), p] * (
@@ -450,20 +484,25 @@
         )
 
     def b_below(w, n, first):
-        hb, hmu = below_earth[0], below_earth[1]
-        vz = below[w, 2]
-        if first:
-            term = hb * state[w, SZZ, 0]
-        else:
-            vx_m, vy_m, szz_m = (low_in[w, n - 1, i] for i in range(3))
+        if not first:
+            hmu = below_earth[1]
+            vx_m, vy_m = low_in[w, n - 1, 0], low_in[w, n - 1, 1]
             sxz = below[w, 0] + hmu * ((state[w, VX, 0] - vx_m) + slope[w, BELOW, 0])
             syz = below[w, 1] + hmu * ((state[w, VY, 0] - vy_m) + slope[w, BELOW, 1])
             below[w, 0] = sxz
             below[w, 1] = syz
-            term = hb * (bx(sxz) + by(syz) + (state[w, SZZ, 0] - szz_m))
-        if w == 1:
-            term = term + inject[n, 0]
-        below[w, 2] = vz + term
+
+        def flat():
+            return None if first else bx(sxz) + by(syz)
+
+        def finish(shear):
+            szz = state[w, SZZ, 0]
+            term = below_earth[0] * (szz if first else shear + (szz - low_in[w, n - 1, 2]))
+            if w == 1:
+                term = term + inject[n, 0]
+            below[w, 2] = below[w, 2] + term
+
+        return flat, finish
 
     def above_velocity(w, sxz, syz):
         hb = above_earth[0]
@@ -472,14 +511,17 @@
         return vx, vy
 
     def above_fast(w, n):
-        sxz, syz, vz = (high_in[w, n - 1, i] for i in range(3))
-        vx, vy = above_velocity(w, sxz, syz)
+        vx, vy = above_velocity(w, high_in[w, n - 1, 0], high_in[w, n - 1, 1])
         above[w, 0] = vx
         above[w, 1] = vy
-        dvz = vz - state[w, VZ, last]
-        szz = widen(w, ABOVE, planes, n - 1, vx, vy, dvz, above_earth[1], above_earth[2], above[w, 4])
-        above[w, 4] = szz
-        return vx, vy, szz
+        change = widen(w, ABOVE, planes, n - 1, vx, vy, above_earth[1], above_earth[2])
+
+        def finish():
+            szz = above[w, 4] + change(high_in[w, n - 1, 2] - state[w, VZ, last])
+            above[w, 4] = szz
+            return szz
+
+        return (vx, vy), finish
 
     def above_slow(w):
         sxx, syy, sxy, _ = rest_of(
@@ -490,6 +532,55 @@
         above[w, 5] = sxy
 
     inner = range(1, last)
+    bounds = [(nx, last * nx), ((planes + 1) * nx, (planes + last - 1) * nx)]
+    early = [i for i in range(2) if bounds[i][1] > bounds[i][0]]
+    bounds += [(0, nx), (last * nx, (planes + 1) * nx), ((planes + last - 1) * nx, 2 * planes * nx)]
+    late = [2, 3, 4]
+    pairs = shot_count // 2 if paired else shot_count
+
+    def piece(i):
+        return pl.ds(bounds[i][0], bounds[i][1] - bounds[i][0])
+
+    def to_shot(src, dst, send, recv, target):
+        return pltpu.make_async_remote_copy(
+            src_ref=src,
+            dst_ref=dst,
+            send_sem=send,
+            recv_sem=recv,
+            device_id={"shot": target},
+            device_id_type=MESH,
+        )
+
+    def gather_pair(i):
+        sems = near_send.at[0, i], near_recv.at[0, i]
+        return to_shot(image.at[piece(i)], near_in.at[piece(i)], *sems, shot + 1)
+
+    def give_back(i):
+        sems = near_send.at[1, i], near_recv.at[1, i]
+        return to_shot(out.at[piece(i)], out.at[piece(i)], *sems, shot - 1)
+
+    def cross(i, k):
+        target = lax.rem(shot + k * (shot_count // pairs), shot_count)
+        sems = cross_send.at[k - 1, i], cross_recv.at[k - 1, i]
+        return to_shot(near_sum.at[piece(i)], cross_in.at[k - 1, piece(i)], *sems, target)
+
+    def merge_pair(i):
+        if paired:
+            gather_pair(i).wait_recv()
+            near_sum[piece(i), :] = image[piece(i), :] + near_in[piece(i), :]
+        else:
+            near_sum[piece(i), :] = image[piece(i), :]
+        for k in range(1, pairs):
+            cross(i, k).start()
+
+    def merge_all(i):
+        total = near_sum[piece(i), :]
+        for k in range(1, pairs):
+            cross(i, k).wait_recv()
+            total = total + cross_in[k - 1, piece(i), :]
+        out[piece(i), :] = total
+        if paired:
+            give_back(i).start()
 
     def run(deep):
         def inside(w, n):
@@ -502,14 +593,39 @@
             for i, value in enumerate(values):
                 buf[w, n, i] = value
 
-        def lowest_down(w, n):
-            values = b_fast(w, 0, LOWEST, n, isinstance(n, int) and n == 0, own_upper(w, 0))
-            store(down_out, values, w, n)
-            wanted = has_low if w == 1 else has_low & (n < steps - 1)
+        def start_up(w, n, part):
+            @pl.when(has_high)
+            def _():
+                send_up(w, n, part).start()
+
+        def start_down(w, n, part):
+            wanted = has_low
+            if deep and (w == 0 or part == 1):
+                wanted = has_low & (n < steps - 1)
 
             @pl.when(wanted)
             def _():
-                send_down(w, n).start()
+                send_down(w, n, part).start()
+
+        def wait_high(w, n, part):
+            @pl.when(has_high)
+            def _():
+                send_down(w, n, part).wait_recv()
+
+        def wait_low(w, n, part):
+            @pl.when(has_low)
+            def _():
+                send_up(w, n, part).wait_recv()
+
+        def first_low(w):
+            @pl.when(has_low)
+            def _():
+                up_first[w].wait_recv()
+                if w == 0:
+                    up_earth[0].wait_recv()
+
+            if w == 0:
+                below_earth[0] = below_earth[0] * h
 
         def half(w, n, first, final):
             if first:
@@ -518,38 +634,21 @@
                 def _():
                     down_first[w].wait_recv()
 
-            else:
-
-                @pl.when(has_high)
-                def _():
-                    send_down(w, n - 1).wait_recv()
-
-            def wait_low():
-                @pl.when(has_low)
-                def _():
-                    if first:
-                        up_first[w].wait_recv()
-                        if w == 0:
-                            up_earth[0].wait_recv()
-                    else:
-                        send_up(w, n - 1).wait_recv()
-
-                if first and w == 0:
-                    below_earth[0] = below_earth[0] * h
-
-            if not deep:
-                wait_low()
-            if first:
-                upper = (None, None, above[w, 4])
-            elif deep:
-                upper = above_fast(w, n)
-            else:
-                upper = tuple(high_in[w, n - 1, i] for i in range(3))
+                szz_f = above[w, 4]
+            vx_f = vy_f = None
             if final:
+                for part in range(2):
+                    wait_high(w, n - 1, part)
+                    wait_low(w, n - 1, part)
                 if deep:
-                    wait_low()
-                b_fast(w, last, LAST, n, first, upper)
-                b_below(w, n, first)
+                    (vx_f, vy_f), lift = above_fast(w, n)
+                    szz_f = lift()
+                else:
+                    vx_f, vy_f, szz_f = (high_in[w, n - 1, i] for i in range(3))
+                _, shear, rise = b_fast(w, last, LAST, n, first, vx_f, vy_f)
+                rise(shear(), szz_f)
+                shear, rise = b_below(w, n, first)
+                rise(shear())
                 if w == 1:
                     keep_twist(last, n)
                     if deep:
@@ -557,30 +656,63 @@
                 a_final(w, 0, n)
                 a_final(w, last, n)
             elif deep:
-                b_fast(w, last, LAST, n, first, upper)
-                store(up_out, a_fast(w, last, n), w, n)
-
-                @pl.when(has_high)
-                def _():
-                    send_up(w, n).start()
-
-                wait_low()
-                b_below(w, n, first)
-                a_fast(w, 0, n)
-                lowest_down(w, n + 1)
+                if not first:
+                    wait_high(w, n - 1, 0)
+                    (vx_f, vy_f), lift = above_fast(w, n)
+                _, shear, rise = b_fast(w, last, LAST, n, first, vx_f, vy_f)
+                values, top = a_fast(w, last, n)
+                store(up_out, values, w, n)
+                start_up(w, n, 0)
+                shear = shear()
+                if not first:
+                    wait_high(w, n - 1, 1)
+                    szz_f = lift()
+                rise(shear, szz_f)
+                up_out[w, n, 2] = top()
+                start_up(w, n, 1)
+                if first:
+                    first_low(w)
+                else:
+                    wait_low(w, n - 1, 0)
+                shear_m, rise_m = b_below(w, n, first)
+                _, bottom = a_fast(w, 0, n)
+                lower = (state[w, VX, 1], state[w, VY, 1])
+                values, shear, rise = b_fast(w, 0, LOWEST, n + 1, False, *lower)
+                store(down_out, values, w, n + 1)
+                start_down(w, n + 1, 0)
+                shear_m, shear = shear_m(), shear()
+                if not first:
+                    wait_low(w, n - 1, 1)
+                rise_m(shear_m)
+                bottom()
+                down_out[w, n + 1, 2] = rise(shear, state[w, SZZ, 1])
+                start_down(w, n + 1, 1)
             else:
-                b_below(w, n, first)
-                b_fast(w, last, LAST, n, first, upper)
-                store(down_out, a_fast(w, 0, n), w, n)
-                store(up_out, a_fast(w, last, n), w, n)
-
-                @pl.when(has_low)
-                def _():
-                    send_down(w, n).start()
-
-                @pl.when(has_high)
-                def _():
-                    send_up(w, n).start()
+                if first:
+                    first_low(w)
+                else:
+                    wait_low(w, n - 1, 0)
+                    wait_high(w, n - 1, 0)
+                    vx_f, vy_f = high_in[w, n - 1, 0], high_in[w, n - 1, 1]
+                shear_m, rise_m = b_below(w, n, first)
+                _, shear, rise = b_fast(w, last, LAST, n, first, vx_f, vy_f)
+                values, bottom = a_fast(w, 0, n)
+                store(down_out, values, w, n)
+                values, top = a_fast(w, last, n)
+                store(up_out, values, w, n)
+                start_down(w, n, 0)
+                start_up(w, n, 0)
+                shear_m, shear = shear_m(), shear()
+                if not first:
+                    wait_low(w, n - 1, 1)
+                    wait_high(w, n - 1, 1)
+                    szz_f = high_in[w, n - 1, 2]
+                rise_m(shear_m)
+                rise(shear, szz_f)
+                down_out[w, n, 2] = bottom()
+                up_out[w, n, 2] = top()
+                start_down(w, n, 1)
+                start_up(w, n, 1)
 
             if not final:
                 if w == 1 and not first:
@@ -610,7 +742,7 @@
                 @pl.when(has_high)
                 def _():
                     if deep:
-                        send_down(1, n).wait_recv()
+                        send_down(1, n, 0).wait_recv()
                     else:
                         send_rest.wait_recv()
 
@@ -621,6 +753,8 @@
                     vx_p = rest_in[0] - hb * state[1, SXZ, last]
                     vy_p = rest_in[1] - hb * state[1, SYZ, last]
                 for p in range(planes):
+                    if 0 < p < last - 1:
+                        continue
                     vx_f = vx_p if p == last else state[1, VX, p + 1]
                     vy_f = vy_p if p == last else state[1, VY, p + 1]
                     vz = state[1, VZ, p]
@@ -628,7 +762,11 @@
 
         for w in range(2):
             if deep:
-                lowest_down(w, 0)
+                values, shear, rise = b_fast(w, 0, LOWEST, 0, True, None, None)
+                store(down_out, values, w, 0)
+                start_down(w, 0, 0)
+                down_out[w, 0, 2] = rise(shear(), state[w, SZZ, 1])
+                start_down(w, 0, 1)
                 set_slope(w, LOWEST, state[w, VZ, 0])
             for p in sorted({0, last}):
                 set_grad(w, edge_at(p), *(state[w, i, p] for i in (SXX, SYY, SXY)))
@@ -659,8 +797,34 @@
             return carry
 
         lax.fori_loop(1, steps - 1, body, 0)
-        for w in range(2):
-            half(w, steps - 1, False, True)
+        for p in range(1, last - 1):
+            vx, vy, vz = (state[1, i, p] for i in (VX, VY, VZ))
+            curl(1, p, steps, state[1, VX, p + 1] - vx, state[1, VY, p + 1] - vy, fx(vz), fy(vz))
+        if deep:
+            for i in early:
+                gather_pair(i).start()
+        half(0, steps - 1, False, True)
+        if not deep:
+            for i in early:
+                merge_pair(i)
+        half(1, steps - 1, False, True)
+        if deep:
+            for i in late:
+                gather_pair(i).start()
+            for i in early + late:
+                give_back(i).wait_recv()
+            for i in early + late:
+                gather_pair(i).wait_send()
+        else:
+            for i in late:
+                merge_pair(i)
+            for i in early + late:
+                merge_all(i)
+            for i in early + late:
+                for k in range(1, pairs):
+                    cross(i, k).wait_send()
+                if paired:
+                    give_back(i).wait_send()
 
     if paired:
         pl.when(far)(lambda: run(True))
@@ -668,45 +832,6 @@
     else:
         run(False)
 
-    total = image.shape[0]
-    chunk = total // shot_count
-
-    def span(index):
-        return pl.ds(pl.multiple_of(index * chunk, 8), chunk)
-
-    scatter = []
-    for k in range(1, shot_count):
-        peer = lax.rem(shot + k, shot_count)
-        copy = pltpu.make_async_remote_copy(
-            src_ref=image.at[span(peer)],
-            dst_ref=parts_in.at[k - 1],
-            send_sem=img_send.at[0, k - 1],
-            recv_sem=img_recv.at[0, k - 1],
-            device_id={"shot": peer},
-            device_id_type=MESH,
-        )
-        copy.start()
-        scatter.append(copy)
-    acc = image[span(shot), :]
-    for k in range(1, shot_count):
-        scatter[k - 1].wait_recv()
-        acc = acc + parts_in[k - 1]
-    own[...] = acc
-    gather = []
-    for k in range(1, shot_count):
-        peer = lax.rem(shot + k, shot_count)
-        copy = pltpu.make_async_remote_copy(
-            src_ref=own,
-            dst_ref=out.at[span(shot)],
-            send_sem=img_send.at[1, k - 1],
-            recv_sem=img_recv.at[1, k - 1],
-            device_id={"shot": peer},
-            device_id_type=MESH,
-        )
-        copy.start()
-        gather.append(copy)
-    out[span(shot), :] = acc
-
     @pl.when(has_high)
     def _():
         for copy in up_first + up_earth:
@@ -728,7 +853,7 @@
         def _():
             for copy in down_far:
                 copy.wait_send()
-            send_down(1, steps - 1).wait_send()
+            send_down(1, steps - 1, 0).wait_send()
 
     if paired:
         pl.when(far)(drain_far)
@@ -741,19 +866,17 @@
 
             @pl.when(has_high)
             def _(w=w):
-                send_up(w, n).wait_send()
+                for part in range(2):
+                    send_up(w, n, part).wait_send()
 
             @pl.when(has_low)
             def _(w=w):
-                send_down(w, n).wait_send()
+                for part in range(2):
+                    send_down(w, n, part).wait_send()
 
         return carry
 
     lax.fori_loop(0, steps - 1, drain, 0)
-    for copy in scatter:
-        copy.wait_send()
-    for copy in gather:
-        copy.wait()
 
 
 def on_device(
@@ -771,7 +894,7 @@
     planes, nx, ny = wavefields.shape[3:]
     steps = wavelet.shape[1]
     rows = 2 * planes * nx
-    peers = max(shot_count - 1, 1)
+    groups = max((shot_count + 1) // 2 - 1, 1)
     f32 = jnp.float32
     vmem = pl.BlockSpec(memory_space=pltpu.VMEM)
     hbm = pl.BlockSpec(memory_space=pltpu.HBM)
@@ -810,8 +933,9 @@
             plane(2, 3, 2),
             plane(2),
             pltpu.VMEM((rows, ny), f32),
-            pltpu.VMEM((peers, rows // shot_count, ny), f32),
-            pltpu.VMEM((rows // shot_count, ny), f32),
+            pltpu.VMEM((rows, ny), f32),
+            pltpu.VMEM((rows, ny), f32),
+            pltpu.VMEM((groups, rows, ny), f32),
             pltpu.SMEM(source_depth.shape, jnp.int32),
             pltpu.SMEM(source_column.shape, jnp.int32),
             pltpu.SMEM(wavelet.shape, f32),
@@ -821,13 +945,15 @@
             dma((18,)),
             dma((13,)),
             dma((13,)),
-            dma((2, steps)),
-            dma((2, steps)),
-            dma((2, steps)),
-            dma((2, steps)),
+            dma((2, steps, 2)),
+            dma((2, steps, 2)),
+            dma((2, steps, 2)),
+            dma((2, steps, 2)),
             dma((2,)),
-            dma((2, peers)),
-            dma((2, peers)),
+            dma((2, 5)),
+            dma((2, 5)),
+            dma((groups, 5)),
+            dma((groups, 5)),
         ],
         compiler_params=pltpu.CompilerParams(collective_id=0, has_side_effects=True),
     )(

time: 36.9 us -> 34.9 us (0.946)
  Pallas kernels: 34.8 us -> 32.8 us
    pallas_call x1, Pallas kernels: 34.8 us -> 32.8 us  [on_device(): pl.pallas_call(functools.partial(kernel, gz_count, shot_count), out_shape...]
where the time goes in v3:
time: 34.9 us; the launch traced here: 34.7 us
  Pallas kernels  32.8 us (94%)
  between operations  1.3 us (4%)
  local copies, waits for them, and re-layouts  0.66 us (2%)
    pallas_call x1, Pallas kernels, on_device(): pl.pallas_call(functools.partial(kernel, gz_count, shot_count), out_shape...  32.8 us

profile of v3, /device:TPU:0, one launch (start us, length us, event | category | flops | bytes accessed | tf_op | source)
XLA Modules:
  0.0 34.7 jit_solution(7712214968285690254)
XLA Ops:
  1.3 32.8 %shard_map.82 = f32[256,128]{1,0:T(8,128)S(1)} custom-call(f32[1,2,9,4,32,128]{5,4,3,2,1,0:T(8,128)} %wave_hbm.1, f32[3,4,32,128]{3,2,1,0:T(8,128)} %earth_hbm.1, s32[1]{0:T(128)S(6)} %copy.11.src_depth_hbm, s32[1]{0:T(128)S(6)} %copy.12.src_column_hbm, f32[1,8]{1,0:T(1,128)} %wavelet_hbm.1, s32[1,64]{1,0:T(1,128)} %rec_depth_hbm.1, s32[1,64]{1,0:T(1,128)} %rec_column_hbm.1, ...), custom_call_target="tpu_custom_call" | custom-call | tf_op jit(solution)/shard_map/pallas_call | solution.py:906
  34.1 0.7 %copy.10 = f32[2,4,32,128]{3,2,1,0:T(8,128)} copy(f32[2,4,32,128]{3,2,1,0:T(8,128)S(1)} %bitcast.1) | data formatting | bytes 262144

commit v4 on v3

--- a/solution.py
+++ b/solution.py
@@ -31,9 +31,10 @@
     above,
     above_earth,
     first_up,
-    first_szz,
-    earth_up,
-    earth_down,
+    first_down,
+    ghost_down,
+    earth_last,
+    earth_first,
     low_in,
     high_in,
     up_out,
@@ -60,14 +61,12 @@
     load_sem,
     init_send,
     init_recv,
-    up_send,
+    step_send,
     up_recv,
-    down_send,
     down_recv,
     rest_sem,
-    near_send,
-    near_recv,
-    cross_send,
+    sum_send,
+    sum_recv,
     cross_recv,
 ):
     planes, nx, ny = state.shape[2:]
@@ -84,22 +83,32 @@
     def local(src, dst, k):
         return pltpu.make_async_copy(src, dst, load_sem.at[k])
 
+    def loaded(dst, k):
+        local(dst, dst, k).wait()
+
     load_first = [
         [
-            local(wave_hbm.at[0, w, pl.ds(SXZ, 2), last], first_up.at[w, pl.ds(0, 2)], 4 * w),
-            local(wave_hbm.at[0, w, SZZ, 0], first_szz.at[w], 4 * w + 1),
-            local(wave_hbm.at[0, w], state.at[w], 4 * w + 2),
+            local(wave_hbm.at[0, w, pl.ds(SXZ, 2), last], first_up.at[w, pl.ds(0, 2)], w),
+            local(wave_hbm.at[0, w, VZ, last], first_up.at[w, 2], w),
+            local(wave_hbm.at[0, w, SZZ, last], first_up.at[w, 3], w),
         ]
         for w in range(2)
     ]
-    load_edge = [
-        local(earth_hbm.at[0, last], earth_up.at[0], 8),
-        local(earth_hbm.at[2, last], earth_up.at[1], 9),
-        local(earth_hbm.at[:, 0], earth_down, 10),
+    load_down = local(wave_hbm.at[0, :, SZZ, 0], first_down, 2)
+    load_ghost = [
+        local(wave_hbm.at[0, :, pl.ds(VX, 2), 0], ghost_down.at[:, pl.ds(0, 2)], 3),
+        local(wave_hbm.at[0, :, pl.ds(SXX, 2), 0], ghost_down.at[:, pl.ds(2, 2)], 3),
+        local(wave_hbm.at[0, :, SXY, 0], ghost_down.at[:, 4], 3),
     ]
-    load_earth = local(earth_hbm, earth, 11)
+    load_state = [local(wave_hbm.at[0, w], state.at[w], 4 + w) for w in range(2)]
+    load_edges = [
+        local(earth_hbm.at[0, last], earth_last.at[0], 6),
+        local(earth_hbm.at[2, last], earth_last.at[1], 6),
+    ]
+    load_lowest = local(earth_hbm.at[:, 0], earth_first, 7)
+    load_earth = local(earth_hbm, earth, 8)
     small = [
-        local(src, dst, 12 + i)
+        local(src, dst, 9 + i)
         for i, (src, dst) in enumerate(
             (
                 (traces_hbm.at[0], traces),
@@ -111,7 +120,9 @@
             )
         )
     ]
-    for copy in load_edge[:1] + load_first[0] + load_first[1] + load_edge[1:] + [load_earth] + small:
+    for copy in load_edges + load_first[0] + [load_down] + load_first[1]:
+        copy.start()
+    for copy in load_ghost + [load_lowest, load_state[0], load_earth] + small + [load_state[1]]:
         copy.start()
 
     barrier = pltpu.get_barrier_semaphore()
@@ -158,68 +169,43 @@
             device_id_type=MESH,
         )
 
-    def initial(src, dst, k, step_to):
-        return remote(src, dst, init_send.at[k], init_recv.at[k], step_to)
-
-    up_first = [initial(first_up.at[w], below.at[w], w, 1) for w in range(2)]
-    up_earth = [initial(earth_up.at[i], below_earth.at[i], 2 + i, 1) for i in range(2)]
-    down_first = [initial(first_szz.at[w], above.at[w, 4], 4 + w, -1) for w in range(2)]
-    down_near = initial(earth_down.at[0], above_earth.at[0], 6, -1)
-    down_far = [
-        initial(earth_down, above_earth, 6, -1),
-    ] + [
-        initial(src, dst, 7 + 3 * w + i, -1)
-        for w in range(2)
-        for i, (src, dst) in enumerate(
-            (
-                (wave_hbm.at[0, w, pl.ds(VX, 2), 0], above.at[w, pl.ds(0, 2)]),
-                (wave_hbm.at[0, w, pl.ds(SXX, 2), 0], above.at[w, pl.ds(2, 2)]),
-                (wave_hbm.at[0, w, SXY, 0], above.at[w, 5]),
-            )
-        )
-    ]
-
+    def initial(src, dst, k, m, step_to):
+        return remote(src, dst, init_send.at[m], init_recv.at[k], step_to)
+
+    up_first = [initial(first_up.at[w, pl.ds(0, 3)], below.at[w], w, 0, 1) for w in range(2)]
+    up_earth = [initial(earth_last.at[k], below_earth.at[k], 2 + k, 1, 1) for k in range(2)]
+    down_first = [initial(first_down.at[w], above.at[w, 5], 4 + w, 2, -1) for w in range(2)]
+    down_near = initial(earth_first.at[0], above_earth.at[0], 6, 3, -1)
+    down_earth = initial(earth_first, above_earth, 6, 3, -1)
+    down_far = [initial(ghost_down.at[w], above.at[w, pl.ds(0, 5)], 7 + w, 4, -1) for w in range(2)]
+
+    loaded(earth_last, 6)
     for w in range(2):
-        if w == 0:
-            load_edge[0].wait()
-        for copy in load_first[w]:
-            copy.wait()
-        szz, vz = state[w, SZZ, last], state[w, VZ, last]
-        first_up[w, 2] = vz + (h * earth_up[0]) * (bx(first_up[w, 0]) + by(first_up[w, 1]) - szz)
+        loaded(first_up.at[w], w)
+        around = bx(first_up[w, 0]) + by(first_up[w, 1]) - first_up[w, 3]
+        first_up[w, 2] = first_up[w, 2] + (h * earth_last[0]) * around
 
         @pl.when(has_high)
         def _(w=w):
             up_first[w].start()
-            if w == 0:
-                up_earth[0].start()
+            up_earth[w].start()
+
+        if w == 0:
+            load_down.wait()
 
         @pl.when(has_low)
         def _(w=w):
             down_first[w].start()
 
-    for copy in load_edge[1:]:
-        copy.wait()
-
-    @pl.when(has_high)
-    def _():
-        up_earth[1].start()
+    load_lowest.wait()
+    loaded(ghost_down, 3)
 
     if paired:
 
         @pl.when(has_low & far)
         def _():
-            for copy in down_far:
-                copy.start()
-
-        @pl.when(has_low & jnp.logical_not(far))
-        def _():
-            down_near.start()
-
-    else:
-
-        @pl.when(has_low)
-        def _():
-            down_near.start()
+            down_far[0].start()
+            down_earth.start()
 
     @pl.when(jnp.logical_not(has_low))
     def _():
@@ -238,9 +224,9 @@
     load_earth.wait()
     earth[...] = earth[...] * h
 
+    offset = gz * planes
     for copy in small:
         copy.wait()
-    offset = gz * planes
     receivers = traces.shape[1]
     column = rec_column[...]
     depth = rec_depth[...] - offset
@@ -263,8 +249,6 @@
         ).reshape(planes + 1, nx, ny)
         return carry
 
-    lax.fori_loop(0, steps, fill, 0)
-
     src_at = src_depth[0] - offset
     src_cell = src_column[0]
 
@@ -274,6 +258,9 @@
 
     def parity(n):
         return n % 2 if isinstance(n, int) else lax.rem(n, 2)
+
+    def mod3(n):
+        return n % 3 if isinstance(n, int) else lax.rem(n, 3)
 
     def part_of(ref, w, n, part):
         return ref.at[w, n, pl.ds(0, 2)] if part == 0 else ref.at[w, n, 2]
@@ -282,8 +269,8 @@
         return remote(
             part_of(up_out, w, n, part),
             part_of(low_in, w, n, part),
-            up_send.at[w, n, part],
-            up_recv.at[w, n, part],
+            step_send.at[0],
+            up_recv.at[w, part, mod3(n)],
             1,
         )
 
@@ -291,8 +278,8 @@
         return remote(
             part_of(down_out, w, n, part),
             part_of(high_in, w, n, part),
-            down_send.at[w, n, part],
-            down_recv.at[w, n, part],
+            step_send.at[1],
+            down_recv.at[w, part, mod3(n)],
             -1,
         )
 
@@ -517,19 +504,19 @@
         change = widen(w, ABOVE, planes, n - 1, vx, vy, above_earth[1], above_earth[2])
 
         def finish():
-            szz = above[w, 4] + change(high_in[w, n - 1, 2] - state[w, VZ, last])
-            above[w, 4] = szz
+            szz = above[w, 5] + change(high_in[w, n - 1, 2] - state[w, VZ, last])
+            above[w, 5] = szz
             return szz
 
         return (vx, vy), finish
 
     def above_slow(w):
         sxx, syy, sxy, _ = rest_of(
-            w, ABOVE, above[w, 0], above[w, 1], above_earth[2], above[w, 2], above[w, 3], above[w, 5]
+            w, ABOVE, above[w, 0], above[w, 1], above_earth[2], above[w, 2], above[w, 3], above[w, 4]
         )
         above[w, 2] = sxx
         above[w, 3] = syy
-        above[w, 5] = sxy
+        above[w, 4] = sxy
 
     inner = range(1, last)
     bounds = [(nx, last * nx), ((planes + 1) * nx, (planes + last - 1) * nx)]
@@ -551,36 +538,47 @@
             device_id_type=MESH,
         )
 
+    def group(i):
+        return 0 if i in early else i - 1
+
     def gather_pair(i):
-        sems = near_send.at[0, i], near_recv.at[0, i]
+        sems = sum_send.at[0], sum_recv.at[group(i)]
         return to_shot(image.at[piece(i)], near_in.at[piece(i)], *sems, shot + 1)
 
     def give_back(i):
-        sems = near_send.at[1, i], near_recv.at[1, i]
+        sems = sum_send.at[1], sum_recv.at[4]
         return to_shot(out.at[piece(i)], out.at[piece(i)], *sems, shot - 1)
 
     def cross(i, k):
         target = lax.rem(shot + k * (shot_count // pairs), shot_count)
-        sems = cross_send.at[k - 1, i], cross_recv.at[k - 1, i]
+        sems = sum_send.at[2], cross_recv.at[k - 1, group(i)]
         return to_shot(near_sum.at[piece(i)], cross_in.at[k - 1, piece(i)], *sems, target)
 
-    def merge_pair(i):
+    def arrived(dst, sem, which):
+        count = sum(bounds[i][1] - bounds[i][0] for i in which)
+        whole = dst.at[pl.ds(0, count)]
+        pltpu.make_async_copy(whole, whole, sem).wait()
+
+    def merge_pair(which):
         if paired:
-            gather_pair(i).wait_recv()
-            near_sum[piece(i), :] = image[piece(i), :] + near_in[piece(i), :]
-        else:
+            arrived(near_in, sum_recv.at[group(which[0])], which)
+        for i in which:
             near_sum[piece(i), :] = image[piece(i), :]
+            if paired:
+                near_sum[piece(i), :] += near_in[piece(i), :]
+            for k in range(1, pairs):
+                cross(i, k).start()
+
+    def merge_all(which):
         for k in range(1, pairs):
-            cross(i, k).start()
-
-    def merge_all(i):
-        total = near_sum[piece(i), :]
-        for k in range(1, pairs):
-            cross(i, k).wait_recv()
-            total = total + cross_in[k - 1, piece(i), :]
-        out[piece(i), :] = total
-        if paired:
-            give_back(i).start()
+            arrived(cross_in.at[k - 1], cross_recv.at[k - 1, group(which[0])], which)
+        for i in which:
+            total = near_sum[piece(i), :]
+            for k in range(1, pairs):
+                total = total + cross_in[k - 1, piece(i), :]
+            out[piece(i), :] = total
+            if paired:
+                give_back(i).start()
 
     def run(deep):
         def inside(w, n):
@@ -599,11 +597,7 @@
                 send_up(w, n, part).start()
 
         def start_down(w, n, part):
-            wanted = has_low
-            if deep and (w == 0 or part == 1):
-                wanted = has_low & (n < steps - 1)
-
-            @pl.when(wanted)
+            @pl.when((has_low & (n < steps - 1)) if deep else has_low)
             def _():
                 send_down(w, n, part).start()
 
@@ -634,7 +628,7 @@
                 def _():
                     down_first[w].wait_recv()
 
-                szz_f = above[w, 4]
+                szz_f = above[w, 5]
             vx_f = vy_f = None
             if final:
                 for part in range(2):
@@ -679,6 +673,13 @@
                 lower = (state[w, VX, 1], state[w, VY, 1])
                 values, shear, rise = b_fast(w, 0, LOWEST, n + 1, False, *lower)
                 store(down_out, values, w, n + 1)
+                if w == 1:
+
+                    @pl.when(has_low & (n == steps - 2))
+                    def _():
+                        rest_out[...] = state[1, SXZ, 0] - state[1, SYZ, 0]
+                        send_rest.start()
+
                 start_down(w, n + 1, 0)
                 shear_m, shear = shear_m(), shear()
                 if not first:
@@ -732,35 +733,45 @@
 
                     @pl.when(has_low & (n == steps - 2))
                     def _():
-                        hb = earth[0, 0]
-                        rest_out[0] = state[1, VX, 0] + hb * (grad[1, 0, 0] + state[1, SXZ, 0])
-                        rest_out[1] = state[1, VY, 0] + hb * (grad[1, 0, 1] + state[1, SYZ, 0])
+                        shear = state[1, SXZ, 0] - state[1, SYZ, 0]
+                        slide = grad[1, 0, 0] - grad[1, 0, 1] + shear
+                        rest_out[...] = state[1, VX, 0] - state[1, VY, 0] + earth[0, 0] * slide
                         send_rest.start()
 
             elif w == 1:
 
                 @pl.when(has_high)
                 def _():
-                    if deep:
-                        send_down(1, n, 0).wait_recv()
-                    else:
-                        send_rest.wait_recv()
-
+                    if not deep:
+                        down_near.wait_recv()
+                    send_rest.wait_recv()
+
+                shear = state[1, SXZ, last] - state[1, SYZ, last]
                 if deep:
-                    vx_p, vy_p = above_velocity(1, high_in[1, n, 0], high_in[1, n, 1])
+                    slide = grad[1, ABOVE, 0] - grad[1, ABOVE, 1] + (rest_in[...] - shear)
+                    gap = above[1, 0] - above[1, 1] + above_earth[0] * slide
                 else:
-                    hb = above_earth[0]
-                    vx_p = rest_in[0] - hb * state[1, SXZ, last]
-                    vy_p = rest_in[1] - hb * state[1, SYZ, last]
+                    gap = rest_in[...] - (above_earth[0] * h) * shear
                 for p in range(planes):
                     if 0 < p < last - 1:
                         continue
-                    vx_f = vx_p if p == last else state[1, VX, p + 1]
-                    vy_f = vy_p if p == last else state[1, VY, p + 1]
-                    vz = state[1, VZ, p]
-                    curl(1, p, n + 1, vx_f - state[1, VX, p], vy_f - state[1, VY, p], fx(vz), fy(vz))
+                    vx, vy, vz = (state[1, i, p] for i in (VX, VY, VZ))
+                    if p == last:
+                        turn = gap - (vx - vy), 0.0
+                    else:
+                        turn = state[1, VX, p + 1] - vx, state[1, VY, p + 1] - vy
+                    curl(1, p, n + 1, *turn, fx(vz), fy(vz))
 
         for w in range(2):
+            load_state[w].wait()
+            if w == 1:
+                if deep:
+
+                    @pl.when(has_low)
+                    def _():
+                        down_far[1].start()
+
+                fill(0, 0)
             if deep:
                 values, shear, rise = b_fast(w, 0, LOWEST, 0, True, None, None)
                 store(down_out, values, w, 0)
@@ -771,6 +782,7 @@
             for p in sorted({0, last}):
                 set_grad(w, edge_at(p), *(state[w, i, p] for i in (SXX, SYY, SXY)))
             inside(w, 0)
+        lax.fori_loop(1, steps, fill, 0)
         for w in range(2):
             half(w, 0, True, False)
 
@@ -780,20 +792,35 @@
 
         below_earth[1] = below_earth[1] * h
 
-        @pl.when(has_high)
-        def _():
-            for copy in down_far if deep else [down_near]:
-                copy.wait_recv()
-
-        for i in range(3 if deep else 1):
-            above_earth[i] = above_earth[i] * h
+        def take_ghost(w):
+            @pl.when(has_high)
+            def _():
+                down_far[w].wait_recv()
+
+            set_grad(w, ABOVE, above[w, 2], above[w, 3], above[w, 4])
+
         if deep:
-            for w in range(2):
-                set_grad(w, ABOVE, above[w, 2], above[w, 3], above[w, 5])
+
+            @pl.when(has_high)
+            def _():
+                down_earth.wait_recv()
+
+            for i in range(3):
+                above_earth[i] = above_earth[i] * h
+            take_ghost(0)
+            if steps == 2:
+                take_ghost(1)
+        else:
+
+            @pl.when(has_low)
+            def _():
+                down_near.start()
 
         def body(n, carry):
-            for w in range(2):
-                half(w, n, False, False)
+            half(0, n, False, False)
+            if deep:
+                pl.when(n == 1)(lambda: take_ghost(1))
+            half(1, n, False, False)
             return carry
 
         lax.fori_loop(1, steps - 1, body, 0)
@@ -805,26 +832,22 @@
                 gather_pair(i).start()
         half(0, steps - 1, False, True)
         if not deep:
-            for i in early:
-                merge_pair(i)
+            merge_pair(early)
         half(1, steps - 1, False, True)
         if deep:
             for i in late:
                 gather_pair(i).start()
-            for i in early + late:
-                give_back(i).wait_recv()
-            for i in early + late:
-                gather_pair(i).wait_send()
+            arrived(out, sum_recv.at[4], early + late)
+            arrived(image, sum_send.at[0], early + late)
         else:
             for i in late:
-                merge_pair(i)
-            for i in early + late:
-                merge_all(i)
-            for i in early + late:
-                for k in range(1, pairs):
-                    cross(i, k).wait_send()
-                if paired:
-                    give_back(i).wait_send()
+                merge_pair([i])
+            for which in [early] + [[i] for i in late]:
+                merge_all(which)
+            for k in range(1, pairs):
+                arrived(near_sum, sum_send.at[2], early + late)
+            if paired:
+                arrived(out, sum_send.at[1], early + late)
 
     if paired:
         pl.when(far)(lambda: run(True))
@@ -832,28 +855,25 @@
     else:
         run(False)
 
+    def left(src, sem):
+        pltpu.make_async_copy(src, src, sem).wait()
+
     @pl.when(has_high)
     def _():
-        for copy in up_first + up_earth:
-            copy.wait_send()
-
-    @pl.when(has_low)
-    def _():
-        for copy in down_first:
-            copy.wait_send()
+        left(below, init_send.at[0])
+        left(earth_last, init_send.at[1])
+        left(up_out.at[:, pl.ds(0, steps - 1)], step_send.at[0])
 
     def drain_near():
         @pl.when(has_low)
         def _():
             down_near.wait_send()
-            send_rest.wait_send()
 
     def drain_far():
         @pl.when(has_low)
         def _():
-            for copy in down_far:
-                copy.wait_send()
-            send_down(1, steps - 1, 0).wait_send()
+            left(ghost_down, init_send.at[4])
+            down_earth.wait_send()
 
     if paired:
         pl.when(far)(drain_far)
@@ -861,22 +881,11 @@
     else:
         drain_near()
 
-    def drain(n, carry):
-        for w in range(2):
-
-            @pl.when(has_high)
-            def _(w=w):
-                for part in range(2):
-                    send_up(w, n, part).wait_send()
-
-            @pl.when(has_low)
-            def _(w=w):
-                for part in range(2):
-                    send_down(w, n, part).wait_send()
-
-        return carry
-
-    lax.fori_loop(0, steps - 1, drain, 0)
+    @pl.when(has_low)
+    def _():
+        left(first_down, init_send.at[2])
+        send_rest.wait_send()
+        left(down_out.at[:, pl.ds(0, steps - 1)], step_send.at[1])
 
 
 def on_device(
@@ -915,16 +924,17 @@
             plane(2),
             plane(2, 6),
             plane(3),
-            plane(2, 3),
+            plane(2, 4),
             plane(2),
+            plane(2, 5),
             plane(2),
             plane(3),
             plane(2, steps, 3),
             plane(2, steps, 3),
             plane(2, steps, 3),
             plane(2, steps, 3),
-            plane(2),
-            plane(2),
+            plane(),
+            plane(),
             plane(steps, planes + 1),
             plane(2, planes),
             plane(planes),
@@ -942,18 +952,16 @@
             pltpu.VMEM(receiver_depth.shape, jnp.int32),
             pltpu.VMEM(receiver_column.shape, jnp.int32),
             pltpu.VMEM(traces.shape[1:], f32),
-            dma((18,)),
-            dma((13,)),
-            dma((13,)),
-            dma((2, steps, 2)),
-            dma((2, steps, 2)),
-            dma((2, steps, 2)),
-            dma((2, steps, 2)),
+            dma((15,)),
+            dma((5,)),
+            dma((9,)),
             dma((2,)),
-            dma((2, 5)),
-            dma((2, 5)),
-            dma((groups, 5)),
-            dma((groups, 5)),
+            dma((2, 2, 3)),
+            dma((2, 2, 3)),
+            dma((2,)),
+            dma((3,)),
+            dma((5,)),
+            dma((groups, 4)),
         ],
         compiler_params=pltpu.CompilerParams(collective_id=0, has_side_effects=True),
     )(

time: 34.9 us -> 33.1 us (0.948)
  Pallas kernels: 32.8 us -> 31 us
    pallas_call x1, Pallas kernels: 32.8 us -> 31 us  [on_device(): pl.pallas_call(functools.partial(kernel, gz_count, shot_count), out_shape...]
where the time goes in v4:
time: 33.1 us; the launch traced here: 33 us
  Pallas kernels  31 us (94%)
  between operations  1.3 us (4%)
  local copies, waits for them, and re-layouts  0.66 us (2%)
    pallas_call x1, Pallas kernels, on_device(): pl.pallas_call(functools.partial(kernel, gz_count, shot_count), out_shape...  31 us

profile of v4, /device:TPU:0, one launch (start us, length us, event | category | flops | bytes accessed | tf_op | source)
XLA Modules:
  0.0 33.0 jit_solution(7018630113967776755)
XLA Ops:
  1.3 31.0 %shard_map.82 = f32[256,128]{1,0:T(8,128)S(1)} custom-call(f32[1,2,9,4,32,128]{5,4,3,2,1,0:T(8,128)} %wave_hbm.1, f32[3,4,32,128]{3,2,1,0:T(8,128)} %earth_hbm.1, s32[1]{0:T(128)S(6)} %copy.11.src_depth_hbm, s32[1]{0:T(128)S(6)} %copy.12.src_column_hbm, f32[1,8]{1,0:T(1,128)} %wavelet_hbm.1, s32[1,64]{1,0:T(1,128)} %rec_depth_hbm.1, s32[1,64]{1,0:T(1,128)} %rec_column_hbm.1, ...), custom_call_target="tpu_custom_call" | custom-call | tf_op jit(solution)/shard_map/pallas_call | solution.py:915
  32.3 0.7 %copy.10 = f32[2,4,32,128]{3,2,1,0:T(8,128)} copy(f32[2,4,32,128]{3,2,1,0:T(8,128)S(1)} %bitcast.1) | data formatting | bytes 262144

commit v5 on v4

--- a/solution.py
+++ b/solution.py
@@ -175,7 +175,17 @@
     up_first = [initial(first_up.at[w, pl.ds(0, 3)], below.at[w], w, 0, 1) for w in range(2)]
     up_earth = [initial(earth_last.at[k], below_earth.at[k], 2 + k, 1, 1) for k in range(2)]
     down_first = [initial(first_down.at[w], above.at[w, 5], 4 + w, 2, -1) for w in range(2)]
-    down_near = initial(earth_first.at[0], above_earth.at[0], 6, 3, -1)
+    if paired:
+        share_near = pltpu.make_async_remote_copy(
+            src_ref=above_earth.at[0],
+            dst_ref=above_earth.at[0],
+            send_sem=init_send.at[5],
+            recv_sem=init_recv.at[6],
+            device_id={"shot": shot + 1},
+            device_id_type=MESH,
+        )
+    else:
+        down_near = initial(earth_first.at[0], above_earth.at[0], 6, 3, -1)
     down_earth = initial(earth_first, above_earth, 6, 3, -1)
     down_far = [initial(ghost_down.at[w], above.at[w, pl.ds(0, 5)], 7 + w, 4, -1) for w in range(2)]
 
@@ -743,7 +753,7 @@
                 @pl.when(has_high)
                 def _():
                     if not deep:
-                        down_near.wait_recv()
+                        pltpu.make_async_copy(rest_in, rest_in, init_recv.at[6]).wait()
                     send_rest.wait_recv()
 
                 shear = state[1, SXZ, last] - state[1, SYZ, last]
@@ -751,7 +761,8 @@
                     slide = grad[1, ABOVE, 0] - grad[1, ABOVE, 1] + (rest_in[...] - shear)
                     gap = above[1, 0] - above[1, 1] + above_earth[0] * slide
                 else:
-                    gap = rest_in[...] - (above_earth[0] * h) * shear
+                    hb = above_earth[0] if paired else above_earth[0] * h
+                    gap = rest_in[...] - hb * shear
                 for p in range(planes):
                     if 0 < p < last - 1:
                         continue
@@ -807,10 +818,15 @@
 
             for i in range(3):
                 above_earth[i] = above_earth[i] * h
+
+            @pl.when(has_high)
+            def _():
+                share_near.start()
+
             take_ghost(0)
             if steps == 2:
                 take_ghost(1)
-        else:
+        elif not paired:
 
             @pl.when(has_low)
             def _():
@@ -865,15 +881,21 @@
         left(up_out.at[:, pl.ds(0, steps - 1)], step_send.at[0])
 
     def drain_near():
-        @pl.when(has_low)
-        def _():
-            down_near.wait_send()
+        if not paired:
+
+            @pl.when(has_low)
+            def _():
+                down_near.wait_send()
 
     def drain_far():
         @pl.when(has_low)
         def _():
             left(ghost_down, init_send.at[4])
             down_earth.wait_send()
+
+        @pl.when(has_high)
+        def _():
+            share_near.wait_send()
 
     if paired:
         pl.when(far)(drain_far)
@@ -953,7 +975,7 @@
             pltpu.VMEM(receiver_column.shape, jnp.int32),
             pltpu.VMEM(traces.shape[1:], f32),
             dma((15,)),
-            dma((5,)),
+            dma((6,)),
             dma((9,)),
             dma((2,)),
             dma((2, 2, 3)),

time: 33.1 us -> 32.9 us (level)
  no operation moved by 1% of the time
where the time goes in v5:
time: 32.9 us; the launch traced here: 32.7 us
  Pallas kernels  30.8 us (94%)
  between operations  1.3 us (4%)
  local copies, waits for them, and re-layouts  0.66 us (2%)
    pallas_call x1, Pallas kernels, on_device(): pl.pallas_call(functools.partial(kernel, gz_count, shot_count), out_shape...  30.8 us

profile of v5, /device:TPU:0, one launch (start us, length us, event | category | flops | bytes accessed | tf_op | source)
XLA Modules:
  0.0 32.7 jit_solution(16692603236492880873)
XLA Ops:
  1.3 30.8 %shard_map.82 = f32[256,128]{1,0:T(8,128)S(1)} custom-call(f32[1,2,9,4,32,128]{5,4,3,2,1,0:T(8,128)} %wave_hbm.1, f32[3,4,32,128]{3,2,1,0:T(8,128)} %earth_hbm.1, s32[1]{0:T(128)S(6)} %copy.11.src_depth_hbm, s32[1]{0:T(128)S(6)} %copy.12.src_column_hbm, f32[1,8]{1,0:T(1,128)} %wavelet_hbm.1, s32[1,64]{1,0:T(1,128)} %rec_depth_hbm.1, s32[1,64]{1,0:T(1,128)} %rec_column_hbm.1, ...), custom_call_target="tpu_custom_call" | custom-call | tf_op jit(solution)/shard_map/pallas_call | solution.py:937
  32.1 0.7 %copy.10 = f32[2,4,32,128]{3,2,1,0:T(8,128)} copy(f32[2,4,32,128]{3,2,1,0:T(8,128)S(1)} %bitcast.1) | data formatting | bytes 262144

commit v6 on v5

--- a/solution.py
+++ b/solution.py
@@ -528,6 +528,41 @@
         above[w, 3] = syy
         above[w, 4] = sxy
 
+    def left(src, sem):
+        pltpu.make_async_copy(src, src, sem).wait()
+
+    def drain_near():
+        if not paired:
+
+            @pl.when(has_low)
+            def _():
+                down_near.wait_send()
+
+    def drain_far():
+        @pl.when(has_low)
+        def _():
+            left(ghost_down, init_send.at[4])
+            down_earth.wait_send()
+
+        @pl.when(has_high)
+        def _():
+            share_near.wait_send()
+
+    def drain(deep):
+        @pl.when(has_high)
+        def _():
+            left(below, init_send.at[0])
+            left(earth_last, init_send.at[1])
+            left(up_out.at[:, pl.ds(0, steps - 1)], step_send.at[0])
+
+        drain_far() if deep else drain_near()
+
+        @pl.when(has_low)
+        def _():
+            left(first_down, init_send.at[2])
+            send_rest.wait_send()
+            left(down_out.at[:, pl.ds(0, steps - 1)], step_send.at[1])
+
     inner = range(1, last)
     bounds = [(nx, last * nx), ((planes + 1) * nx, (planes + last - 1) * nx)]
     early = [i for i in range(2) if bounds[i][1] > bounds[i][0]]
@@ -853,9 +888,11 @@
         if deep:
             for i in late:
                 gather_pair(i).start()
+            drain(True)
             arrived(out, sum_recv.at[4], early + late)
             arrived(image, sum_send.at[0], early + late)
         else:
+            drain(False)
             for i in late:
                 merge_pair([i])
             for which in [early] + [[i] for i in late]:
@@ -870,44 +907,6 @@
         pl.when(jnp.logical_not(far))(lambda: run(False))
     else:
         run(False)
-
-    def left(src, sem):
-        pltpu.make_async_copy(src, src, sem).wait()
-
-    @pl.when(has_high)
-    def _():
-        left(below, init_send.at[0])
-        left(earth_last, init_send.at[1])
-        left(up_out.at[:, pl.ds(0, steps - 1)], step_send.at[0])
-
-    def drain_near():
-        if not paired:
-
-            @pl.when(has_low)
-            def _():
-                down_near.wait_send()
-
-    def drain_far():
-        @pl.when(has_low)
-        def _():
-            left(ghost_down, init_send.at[4])
-            down_earth.wait_send()
-
-        @pl.when(has_high)
-        def _():
-            share_near.wait_send()
-
-    if paired:
-        pl.when(far)(drain_far)
-        pl.when(jnp.logical_not(far))(drain_near)
-    else:
-        drain_near()
-
-    @pl.when(has_low)
-    def _():
-        left(first_down, init_send.at[2])
-        send_rest.wait_send()
-        left(down_out.at[:, pl.ds(0, steps - 1)], step_send.at[1])
 
 
 def on_device(

time: 32.9 us -> 32.9 us (level)
  no operation moved by 1% of the time
where the time goes in v6:
time: 32.9 us; the launch traced here: 32.7 us
  Pallas kernels  30.8 us (94%)
  between operations  1.3 us (4%)
  local copies, waits for them, and re-layouts  0.66 us (2%)
    pallas_call x1, Pallas kernels, on_device(): pl.pallas_call(functools.partial(kernel, gz_count, shot_count), out_shape...  30.8 us

profile of v6, /device:TPU:0, one launch (start us, length us, event | category | flops | bytes accessed | tf_op | source)
XLA Modules:
  0.0 32.7 jit_solution(8738433915276783269)
XLA Ops:
  1.3 30.8 %shard_map.82 = f32[256,128]{1,0:T(8,128)S(1)} custom-call(f32[1,2,9,4,32,128]{5,4,3,2,1,0:T(8,128)} %wave_hbm.1, f32[3,4,32,128]{3,2,1,0:T(8,128)} %earth_hbm.1, s32[1]{0:T(128)S(6)} %copy.11.src_depth_hbm, s32[1]{0:T(128)S(6)} %copy.12.src_column_hbm, f32[1,8]{1,0:T(1,128)} %wavelet_hbm.1, s32[1,64]{1,0:T(1,128)} %rec_depth_hbm.1, s32[1,64]{1,0:T(1,128)} %rec_column_hbm.1, ...), custom_call_target="tpu_custom_call" | custom-call | tf_op jit(solution)/shard_map/pallas_call | solution.py:936
  32.1 0.7 %copy.10 = f32[2,4,32,128]{3,2,1,0:T(8,128)} copy(f32[2,4,32,128]{3,2,1,0:T(8,128)S(1)} %bitcast.1) | data formatting | bytes 262144
